TPU v7x, 32 devices: a whole 2x2x4 slice. The times are simulated.
32 devices in a mesh: chain: 32 (over z, y, x, core).
Axes of the slice: x: 2, y: 2, z: 4, core: 2. Of those that a mesh axis runs over, the one named last changes fastest.
Arguments:
- right_side: float32 [8, 4096], P(None, 'chain'), may hold values from -6 to 6
- diag_block: float32 [8, 8, 4096], P(None, None, 'chain'), may hold values from -2 to 2
- below_block: float32 [8, 8, 4096], P(None, None, 'chain'), may hold values from -2 to 2
- above_block: float32 [8, 8, 4096], P(None, None, 'chain'), may hold values from -2 to 2
- lower_level: float32 [12, 8, 8, 4096], P(None, None, None, 'chain'), may hold values from -0.5 to 0.5
- upper_level: float32 [12, 8, 8, 4096], P(None, None, None, 'chain'), may hold values from -0.5 to 0.5
- final_block: float32 [8, 8, 4096], P(None, None, 'chain'), may hold values from -1 to 1
Outputs:
- basis: float32 [4, 8, 4096], P(None, None, 'chain')
- hess: float32 [4, 3], replicated
All inputs are finite; a program needn't handle non-finite values.
Results may differ from a plain program's by a relative error of at most 0.0001.
Values sent between devices are 32-bit elements; how exact they have to be, the bound alone decides.
No kernel may reach another device: no remote copies, remote signals or barrier semaphores. Data moves between devices by JAX's collectives and lax.ppermute only.
A program may use at most 64 MiB of HBM per device.

v0:
```python
import jax
import jax.numpy as jnp
from jax import lax
from jax.sharding import PartitionSpec as P

ITERS = 3


EPS = 1e-06


def padded_2(x, sides, width):
    for axis, dim in sides:
        peers, length = (lax.axis_size(axis), x.shape[dim])
        up = [(i, (i + 1) % peers) for i in range(peers - 1)]
        down = [(j, i) for i, j in up]
        last = lax.slice_in_dim(x, length - width, length, axis=dim)
        initial = lax.slice_in_dim(x, 0, width, axis=dim)
        before = lax.ppermute(last, axis, up)
        after = lax.ppermute(initial, axis, down)
        x = jnp.concatenate([before, x, after], axis=dim)
    return x


def from_behind(x, axis, by):
    peers = lax.axis_size(axis)
    pairs = [(i, i + by) for i in range(peers) if 0 <= i + by < peers]
    return lax.ppermute(x, axis, pairs)


def blockmul(blocks, field):
    return jnp.einsum("abi,bi->ai", blocks, field, precision=lax.Precision.HIGHEST)


def on_device(
    right_side, diag_block, below_block, above_block, lower_level, upper_level, final_block
):
    rows_here = right_side.shape[1]
    devices = lax.axis_size("chain")
    whole = rows_here * devices
    count = right_side.shape[0] * whole
    depth = lower_level.shape[0]
    near = [level for level in range(depth) if 2**level < rows_here]
    far = [level for level in range(depth) if 2**level >= rows_here and 2**level < whole]
    reach = sum((2**level for level in near))
    stacked_coef = jnp.concatenate([lower_level[: len(near)], upper_level[: len(near)]], 0)
    wide_coef = padded_2(stacked_coef, (("chain", 3),), reach)
    start_sum = lax.psum(jnp.sum(right_side * right_side), "chain")
    basis = [right_side / jnp.sqrt(start_sum / count + EPS)]
    hess = jnp.zeros((ITERS + 1, ITERS), jnp.float32)
    for column in range(ITERS):
        precondition_field = basis[column]
        current = padded_2(precondition_field, (("chain", 1),), reach)
        offset = 0
        for position in range(len(near)):
            stride = 2 ** near[position]
            length = current.shape[1]
            first_col = offset + stride
            last_col = offset + length - stride
            low_coef = wide_coef[position][:, :, first_col:last_col]
            high_coef = wide_coef[len(near) + position][:, :, first_col:last_col]
            current = (
                current[:, stride : length - stride]
                + blockmul(low_coef, current[:, : length - 2 * stride])
                + blockmul(high_coef, current[:, 2 * stride :])
            )
            offset = first_col
        precondition_field = current
        for precondition_level in far:
            hops = 2**precondition_level // rows_here
            below_rows = from_behind(precondition_field, "chain", hops)
            above_rows = from_behind(precondition_field, "chain", -hops)
            precondition_field = (
                precondition_field
                + blockmul(lower_level[precondition_level], below_rows)
                + blockmul(upper_level[precondition_level], above_rows)
            )
        field = precondition_field + blockmul(final_block, precondition_field)
        padded = padded_2(field, (("chain", 1),), 1)
        result = 2.0 * field + blockmul(diag_block, field)
        result = result + blockmul(below_block, padded[:, :rows_here])
        vector = result + blockmul(above_block, padded[:, 2:])
        stacked = jnp.stack(basis)
        local_dots = jnp.einsum("kai,ai->k", stacked, vector, precision=lax.Precision.HIGHEST)
        dots = lax.psum(local_dots, "chain") / count
        vector = vector - jnp.einsum("k,kai->ai", dots, stacked, precision=lax.Precision.HIGHEST)
        squares = lax.psum(jnp.sum(vector * vector), "chain") / count
        length = jnp.sqrt(squares + EPS)
        basis.append(vector / length)
        hess = hess.at[: column + 1, column].set(dots).at[column + 1, column].set(length)
    return (jnp.stack(basis), hess)


def solution(mesh):
    return jax.shard_map(
        on_device,
        mesh=mesh,
        in_specs=(
            P(None, "chain"),
            P(None, None, "chain"),
            P(None, None, "chain"),
            P(None, None, "chain"),
            P(None, None, None, "chain"),
            P(None, None, None, "chain"),
            P(None, None, "chain"),
        ),
        out_specs=(P(None, None, "chain"), P()),
        check_vma=False,
    )
```

profile of v0, /device:TPU:0, one launch (start us, length us, event | category | flops | bytes accessed | tf_op | source)
XLA Modules:
  0.0 513.5 jit_solution(4415420418864798373)
XLA Ops:
  2.8 2.4 collective-permute-start.2
  5.8 1.3 collective-permute-start.3
  7.1 47.2 %psum.49 = f32[]{:T(128)} all-reduce(f32[]{:T(128)} %multiply_reduce_fusion.58), channel_id=1, replica_groups=mesh['chain'=32] {'chain'}, use_global_device_ids=true, to_apply=%region_1.0 | all-reduce | flops 1 | bytes 8 | tf_op jit(solution)/shard_map/psum | solution.py:48
  55.1 1.3 collective-permute-start
  56.4 1.3 collective-permute-start.1
  57.7 4.3 collective-permute-done.1
  65.2 1.3 collective-permute-start.5
  66.5 4.9 collective-permute-start.4
  72.3 1.3 collective-permute-start.7
  73.6 6.4 %collective-permute-start.6 = (f32[8,128]{1,0:T(8,128)S(1)}, f32[8,128]{1,0:T(8,128)S(1)}, u32[]{:S(2)}, u32[]{:S(2)}) collective-permute-start(f32[8,128]{1,0:T(8,128)S(1)} %bitcast_add_fusion.40), channel_id=1, source_target_pairs={{0,2},{1,3},{2,4},{3,5},{4,6},{5,7},{6,8},{7,9},{8,10},{9,11},{10,... | collective-permute-start | bytes 12296 | tf_op jit(solution)/shard_map/ppermute | solution.py:28
  80.0 1.3 collective-permute-done.6
  81.3 1.3 collective-permute-start.9
  82.6 8.6 %collective-permute-start.8 = (f32[8,128]{1,0:T(8,128)S(1)}, f32[8,128]{1,0:T(8,128)S(1)}, u32[]{:S(2)}, u32[]{:S(2)}) collective-permute-start(f32[8,128]{1,0:T(8,128)S(1)} %bitcast_add_fusion.38), channel_id=1, source_target_pairs={{0,4},{1,5},{2,6},{3,7},{4,8},{5,9},{6,10},{7,11},{8,12},{9,13},{1... | collective-permute-start | bytes 12296 | tf_op jit(solution)/shard_map/ppermute | solution.py:28
  91.2 1.3 collective-permute-done.8
  92.5 1.3 collective-permute-start.11
  93.8 7.5 %collective-permute-start.10 = (f32[8,128]{1,0:T(8,128)S(1)}, f32[8,128]{1,0:T(8,128)S(1)}, u32[]{:S(2)}, u32[]{:S(2)}) collective-permute-start(f32[8,128]{1,0:T(8,128)S(1)} %bitcast_add_fusion.36), channel_id=1, source_target_pairs={{0,8},{1,9},{2,10},{3,11},{4,12},{5,13},{6,14},{7,15},{8,16},{9,17... | collective-permute-start | bytes 12296 | tf_op jit(solution)/shard_map/ppermute | solution.py:28
  101.4 1.3 collective-permute-done.10
  102.7 1.3 collective-permute-start.13
  104.0 5.6 %collective-permute-start.12 = (f32[8,128]{1,0:T(8,128)S(1)}, f32[8,128]{1,0:T(8,128)S(1)}, u32[]{:S(2)}, u32[]{:S(2)}) collective-permute-start(f32[8,128]{1,0:T(8,128)S(1)} %bitcast_add_fusion.34), channel_id=1, source_target_pairs={{0,16},{1,17},{2,18},{3,19},{4,20},{5,21},{6,22},{7,23},{8,24},{9,... | collective-permute-start | bytes 12296 | tf_op jit(solution)/shard_map/ppermute | solution.py:28
  109.7 1.3 collective-permute-done.12
  112.4 1.3 collective-permute-start.15
  113.7 2.7 collective-permute-done.15
  117.1 44.6 %psum.50 = f32[1]{0:T(128)} all-reduce(f32[1]{0:T(128)} %bitcast.231), channel_id=1, replica_groups=mesh['chain'=32] {'chain'}, use_global_device_ids=true, to_apply=%region_2.0 | all-reduce | flops 1 | bytes 8 | tf_op jit(solution)/shard_map/psum | solution.py:85
  163.1 40.2 %psum.51 = f32[]{:T(128)} all-reduce(f32[]{:T(128)} %multiply_reduce_fusion.57), channel_id=1, replica_groups=mesh['chain'=32] {'chain'}, use_global_device_ids=true, to_apply=%region_4.0 | all-reduce | flops 1 | bytes 8 | tf_op jit(solution)/shard_map/psum | solution.py:87
  204.1 1.3 collective-permute-start.16
  205.3 1.3 collective-permute-start.17
  206.7 4.3 collective-permute-done.17
  213.5 1.3 collective-permute-start.19
  214.8 4.9 collective-permute-start.18
  220.5 1.3 collective-permute-start.21
  221.8 6.4 %collective-permute-start.20 = (f32[8,128]{1,0:T(8,128)S(1)}, f32[8,128]{1,0:T(8,128)S(1)}, u32[]{:S(2)}, u32[]{:S(2)}) collective-permute-start(f32[8,128]{1,0:T(8,128)S(1)} %bitcast_add_fusion.26), channel_id=1, source_target_pairs={{0,2},{1,3},{2,4},{3,5},{4,6},{5,7},{6,8},{7,9},{8,10},{9,11},{10,... | collective-permute-start | bytes 12296 | tf_op jit(solution)/shard_map/ppermute | solution.py:28
  229.5 1.3 collective-permute-start.23
  230.8 8.6 %collective-permute-start.22 = (f32[8,128]{1,0:T(8,128)S(1)}, f32[8,128]{1,0:T(8,128)S(1)}, u32[]{:S(2)}, u32[]{:S(2)}) collective-permute-start(f32[8,128]{1,0:T(8,128)S(1)} %bitcast_add_fusion.24), channel_id=1, source_target_pairs={{0,4},{1,5},{2,6},{3,7},{4,8},{5,9},{6,10},{7,11},{8,12},{9,13},{1... | collective-permute-start | bytes 12296 | tf_op jit(solution)/shard_map/ppermute | solution.py:28
  240.8 8.3 %collective-permute-start.24 = (f32[8,128]{1,0:T(8,128)S(1)}, f32[8,128]{1,0:T(8,128)S(1)}, u32[]{:S(2)}, u32[]{:S(2)}) collective-permute-start(f32[8,128]{1,0:T(8,128)S(1)} %bitcast_add_fusion.22), channel_id=1, source_target_pairs={{0,8},{1,9},{2,10},{3,11},{4,12},{5,13},{6,14},{7,15},{8,16},{9,17... | collective-permute-start | bytes 12296 | tf_op jit(solution)/shard_map/ppermute | solution.py:28
  249.1 1.3 collective-permute-start.25
  250.4 4.2 collective-permute-done.25
  254.6 1.3 collective-permute-start.27
  255.9 5.4 %collective-permute-start.26 = (f32[8,128]{1,0:T(8,128)S(1)}, f32[8,128]{1,0:T(8,128)S(1)}, u32[]{:S(2)}, u32[]{:S(2)}) collective-permute-start(f32[8,128]{1,0:T(8,128)S(1)} %bitcast_add_fusion.20), channel_id=1, source_target_pairs={{0,16},{1,17},{2,18},{3,19},{4,20},{5,21},{6,22},{7,23},{8,24},{9,... | collective-permute-start | bytes 12296 | tf_op jit(solution)/shard_map/ppermute | solution.py:28
  264.1 1.3 collective-permute-start.29
  265.5 2.3 collective-permute-done.29
  268.8 44.1 %psum.52 = f32[2]{0:T(128)S(1)} all-reduce(f32[2]{0:T(128)S(1)} %convolution_bitcast_fusion.1), channel_id=1, replica_groups=mesh['chain'=32] {'chain'}, use_global_device_ids=true, to_apply=%region_5.0 | all-reduce | flops 2 | bytes 16 | tf_op jit(solution)/shard_map/psum | solution.py:85
  313.6 40.0 %psum.53 = f32[]{:T(128)} all-reduce(f32[]{:T(128)} %get-tuple-element.78), channel_id=1, replica_groups=mesh['chain'=32] {'chain'}, use_global_device_ids=true, to_apply=%region_7.0 | all-reduce | flops 1 | bytes 8 | tf_op jit(solution)/shard_map/psum | solution.py:87
  355.7 1.3 collective-permute-start.31
  357.6 3.6 collective-permute-done.31
  363.7 1.3 collective-permute-start.33
  365.0 4.9 collective-permute-start.32
  370.8 1.3 collective-permute-start.35
  373.4 6.4 %collective-permute-start.34 = (f32[8,128]{1,0:T(8,128)S(1)}, f32[8,128]{1,0:T(8,128)S(1)}, u32[]{:S(2)}, u32[]{:S(2)}) collective-permute-start(f32[8,128]{1,0:T(8,128)S(1)} %bitcast_add_fusion.12), channel_id=1, source_target_pairs={{0,2},{1,3},{2,4},{3,5},{4,6},{5,7},{6,8},{7,9},{8,10},{9,11},{10,... | collective-permute-start | bytes 12296 | tf_op jit(solution)/shard_map/ppermute | solution.py:28
  381.1 1.3 collective-permute-start.37
  382.4 8.6 %collective-permute-start.36 = (f32[8,128]{1,0:T(8,128)S(1)}, f32[8,128]{1,0:T(8,128)S(1)}, u32[]{:S(2)}, u32[]{:S(2)}) collective-permute-start(f32[8,128]{1,0:T(8,128)S(1)} %bitcast_add_fusion.10), channel_id=1, source_target_pairs={{0,4},{1,5},{2,6},{3,7},{4,8},{5,9},{6,10},{7,11},{8,12},{9,13},{1... | collective-permute-start | bytes 12296 | tf_op jit(solution)/shard_map/ppermute | solution.py:28
  392.4 8.3 %collective-permute-start.38 = (f32[8,128]{1,0:T(8,128)S(1)}, f32[8,128]{1,0:T(8,128)S(1)}, u32[]{:S(2)}, u32[]{:S(2)}) collective-permute-start(f32[8,128]{1,0:T(8,128)S(1)} %bitcast_add_fusion.8), channel_id=1, source_target_pairs={{0,8},{1,9},{2,10},{3,11},{4,12},{5,13},{6,14},{7,15},{8,16},{9,17... | collective-permute-start | bytes 12296 | tf_op jit(solution)/shard_map/ppermute | solution.py:28
  400.7 1.9 broadcast_select_fusion.1
  402.6 1.3 collective-permute-start.39
  403.9 4.2 collective-permute-done.39
  408.1 1.3 collective-permute-start.41
  409.4 1.4 scatter.24
  410.8 5.4 %collective-permute-start.40 = (f32[8,128]{1,0:T(8,128)S(1)}, f32[8,128]{1,0:T(8,128)S(1)}, u32[]{:S(2)}, u32[]{:S(2)}) collective-permute-start(f32[8,128]{1,0:T(8,128)S(1)} %bitcast_add_fusion.6), channel_id=1, source_target_pairs={{0,16},{1,17},{2,18},{3,19},{4,20},{5,21},{6,22},{7,23},{8,24},{9,... | collective-permute-start | bytes 12296 | tf_op jit(solution)/shard_map/ppermute | solution.py:28
  417.7 1.3 collective-permute-start.42
  419.0 1.3 collective-permute-start.43
  420.3 2.3 collective-permute-done.43
  423.0 44.2 %psum.54 = f32[3]{0:T(128)S(1)} all-reduce(f32[3]{0:T(128)S(1)} %convolution_bitcast_fusion), channel_id=1, replica_groups=mesh['chain'=32] {'chain'}, use_global_device_ids=true, to_apply=%region_8.0 | all-reduce | flops 3 | bytes 24 | tf_op jit(solution)/shard_map/psum | solution.py:85
  467.3 2.0 broadcast_select_fusion
  469.4 1.4 scatter.26
  471.4 40.0 %psum.55 = f32[]{:T(128)} all-reduce(f32[]{:T(128)} %get-tuple-element.76), channel_id=1, replica_groups=mesh['chain'=32] {'chain'}, use_global_device_ids=true, to_apply=%region_10.0 | all-reduce | flops 1 | bytes 8 | tf_op jit(solution)/shard_map/psum | solution.py:87
  (242 shorter events, 33.3 us)
Async XLA Ops:
  0.6 4.6 copy-start.6
  2.8 59.3 %collective-permute-start.2 = (f32[14,8,8,127]{3,2,1,0:T(8,128)S(1)}, f32[14,8,8,127]{3,2,1,0:T(8,128)S(1)}, u32[]{:S(2)}, u32[]{:S(2)}) collective-permute-start(f32[14,8,8,127]{3,2,1,0:T(8,128)S(1)} %get-tuple-element.96), channel_id=1, source_target_pairs={{0,1},{1,2},{2,3},{3,4},{4,5},{5,6},{6,7},{7,8},{8,9},{9,10},{10,1... | collective-permute-start | bytes 1365512 | tf_op jit(solution)/shard_map/ppermute | solution.py:19
  5.8 56.3 %collective-permute-start.3 = (f32[14,8,8,127]{3,2,1,0:T(8,128)S(1)}, f32[14,8,8,127]{3,2,1,0:T(8,128)S(1)}, u32[]{:S(2)}, u32[]{:S(2)}) collective-permute-start(f32[14,8,8,127]{3,2,1,0:T(8,128)S(1)} %get-tuple-element.97), channel_id=1, source_target_pairs={{1,0},{2,1},{3,2},{4,3},{5,4},{6,5},{7,6},{8,7},{9,8},{10,9},{11,1... | collective-permute-start | bytes 1365512 | tf_op jit(solution)/shard_map/ppermute | solution.py:20
  55.1 2.6 collective-permute-start
  56.4 5.6 %collective-permute-start.1 = (f32[8,127]{1,0:T(8,128)S(1)}, f32[8,127]{1,0:T(8,128)S(1)}, u32[]{:S(2)}, u32[]{:S(2)}) collective-permute-start(f32[8,127]{1,0:T(8,128)S(1)} %get-tuple-element.157), channel_id=1, source_target_pairs={{1,0},{2,1},{3,2},{4,3},{5,4},{6,5},{7,6},{8,7},{9,8},{10,9},{11,1... | collective-permute-start | bytes 12200 | tf_op jit(solution)/shard_map/ppermute | solution.py:20
  62.7 8.7 %copy-start = (f32[12,8,8,128]{3,2,1,0:T(8,128)S(1)}, f32[12,8,8,128]{3,2,1,0:T(8,128)}, u32[]{:S(2)}) copy-start(f32[12,8,8,128]{3,2,1,0:T(8,128)} %param.24) | copy-start | bytes 1179652
  62.8 9.5 %copy-start.1 = (f32[12,8,8,128]{3,2,1,0:T(8,128)S(1)}, f32[12,8,8,128]{3,2,1,0:T(8,128)}, u32[]{:S(2)}) copy-start(f32[12,8,8,128]{3,2,1,0:T(8,128)} %param.23) | copy-start | bytes 1179652
  62.8 48.2 %copy-start.2 = (f32[8,8,128]{2,1,0:T(8,128)S(1)}, f32[8,8,128]{2,1,0:T(8,128)}, u32[]{:S(2)}) copy-start(f32[8,8,128]{2,1,0:T(8,128)} %param.25) | copy-start | bytes 98308
  62.8 50.9 %copy-start.3 = (f32[8,8,128]{2,1,0:T(8,128)S(1)}, f32[8,8,128]{2,1,0:T(8,128)}, u32[]{:S(2)}) copy-start(f32[8,8,128]{2,1,0:T(8,128)} %param.20) | copy-start | bytes 98308
  62.8 53.7 %copy-start.4 = (f32[8,8,128]{2,1,0:T(8,128)S(1)}, f32[8,8,128]{2,1,0:T(8,128)}, u32[]{:S(2)}) copy-start(f32[8,8,128]{2,1,0:T(8,128)} %param.22) | copy-start | bytes 98308
  62.8 53.7 %copy-start.5 = (f32[8,8,128]{2,1,0:T(8,128)S(1)}, f32[8,8,128]{2,1,0:T(8,128)}, u32[]{:S(2)}) copy-start(f32[8,8,128]{2,1,0:T(8,128)} %param.21) | copy-start | bytes 98308
  65.2 6.2 %collective-permute-start.5 = (f32[8,128]{1,0:T(8,128)S(1)}, f32[8,128]{1,0:T(8,128)S(1)}, u32[]{:S(2)}, u32[]{:S(2)}) collective-permute-start(f32[8,128]{1,0:T(8,128)S(1)} %fusion.62), channel_id=1, source_target_pairs={{1,0},{2,1},{3,2},{4,3},{5,4},{6,5},{7,6},{8,7},{9,8},{10,9},{11,1... | collective-permute-start | bytes 12296 | tf_op jit(solution)/shard_map/ppermute | solution.py:28
  66.5 5.7 %collective-permute-start.4 = (f32[8,128]{1,0:T(8,128)S(1)}, f32[8,128]{1,0:T(8,128)S(1)}, u32[]{:S(2)}, u32[]{:S(2)}) collective-permute-start(f32[8,128]{1,0:T(8,128)S(1)} %fusion.62), channel_id=1, source_target_pairs={{0,1},{1,2},{2,3},{3,4},{4,5},{5,6},{6,7},{7,8},{8,9},{9,10},{10,1... | collective-permute-start | bytes 12296 | tf_op jit(solution)/shard_map/ppermute | solution.py:28
  72.3 7.7 %collective-permute-start.7 = (f32[8,128]{1,0:T(8,128)S(1)}, f32[8,128]{1,0:T(8,128)S(1)}, u32[]{:S(2)}, u32[]{:S(2)}) collective-permute-start(f32[8,128]{1,0:T(8,128)S(1)} %bitcast_add_fusion.40), channel_id=1, source_target_pairs={{2,0},{3,1},{4,2},{5,3},{6,4},{7,5},{8,6},{9,7},{10,8},{11,9},{12,... | collective-permute-start | bytes 12296 | tf_op jit(solution)/shard_map/ppermute | solution.py:28
  73.6 7.7 %collective-permute-start.6 = (f32[8,128]{1,0:T(8,128)S(1)}, f32[8,128]{1,0:T(8,128)S(1)}, u32[]{:S(2)}, u32[]{:S(2)}) collective-permute-start(f32[8,128]{1,0:T(8,128)S(1)} %bitcast_add_fusion.40), channel_id=1, source_target_pairs={{0,2},{1,3},{2,4},{3,5},{4,6},{5,7},{6,8},{7,9},{8,10},{9,11},{10,... | collective-permute-start | bytes 12296 | tf_op jit(solution)/shard_map/ppermute | solution.py:28
  81.3 9.9 %collective-permute-start.9 = (f32[8,128]{1,0:T(8,128)S(1)}, f32[8,128]{1,0:T(8,128)S(1)}, u32[]{:S(2)}, u32[]{:S(2)}) collective-permute-start(f32[8,128]{1,0:T(8,128)S(1)} %bitcast_add_fusion.38), channel_id=1, source_target_pairs={{4,0},{5,1},{6,2},{7,3},{8,4},{9,5},{10,6},{11,7},{12,8},{13,9},{1... | collective-permute-start | bytes 12296 | tf_op jit(solution)/shard_map/ppermute | solution.py:28
  82.6 9.9 %collective-permute-start.8 = (f32[8,128]{1,0:T(8,128)S(1)}, f32[8,128]{1,0:T(8,128)S(1)}, u32[]{:S(2)}, u32[]{:S(2)}) collective-permute-start(f32[8,128]{1,0:T(8,128)S(1)} %bitcast_add_fusion.38), channel_id=1, source_target_pairs={{0,4},{1,5},{2,6},{3,7},{4,8},{5,9},{6,10},{7,11},{8,12},{9,13},{1... | collective-permute-start | bytes 12296 | tf_op jit(solution)/shard_map/ppermute | solution.py:28
  92.5 8.9 %collective-permute-start.11 = (f32[8,128]{1,0:T(8,128)S(1)}, f32[8,128]{1,0:T(8,128)S(1)}, u32[]{:S(2)}, u32[]{:S(2)}) collective-permute-start(f32[8,128]{1,0:T(8,128)S(1)} %bitcast_add_fusion.36), channel_id=1, source_target_pairs={{8,0},{9,1},{10,2},{11,3},{12,4},{13,5},{14,6},{15,7},{16,8},{17,9... | collective-permute-start | bytes 12296 | tf_op jit(solution)/shard_map/ppermute | solution.py:28
  93.8 8.9 %collective-permute-start.10 = (f32[8,128]{1,0:T(8,128)S(1)}, f32[8,128]{1,0:T(8,128)S(1)}, u32[]{:S(2)}, u32[]{:S(2)}) collective-permute-start(f32[8,128]{1,0:T(8,128)S(1)} %bitcast_add_fusion.36), channel_id=1, source_target_pairs={{0,8},{1,9},{2,10},{3,11},{4,12},{5,13},{6,14},{7,15},{8,16},{9,17... | collective-permute-start | bytes 12296 | tf_op jit(solution)/shard_map/ppermute | solution.py:28
  102.7 6.9 %collective-permute-start.13 = (f32[8,128]{1,0:T(8,128)S(1)}, f32[8,128]{1,0:T(8,128)S(1)}, u32[]{:S(2)}, u32[]{:S(2)}) collective-permute-start(f32[8,128]{1,0:T(8,128)S(1)} %bitcast_add_fusion.34), channel_id=1, source_target_pairs={{16,0},{17,1},{18,2},{19,3},{20,4},{21,5},{22,6},{23,7},{24,8},{25... | collective-permute-start | bytes 12296 | tf_op jit(solution)/shard_map/ppermute | solution.py:28
  104.0 6.9 %collective-permute-start.12 = (f32[8,128]{1,0:T(8,128)S(1)}, f32[8,128]{1,0:T(8,128)S(1)}, u32[]{:S(2)}, u32[]{:S(2)}) collective-permute-start(f32[8,128]{1,0:T(8,128)S(1)} %bitcast_add_fusion.34), channel_id=1, source_target_pairs={{0,16},{1,17},{2,18},{3,19},{4,20},{5,21},{6,22},{7,23},{8,24},{9,... | collective-permute-start | bytes 12296 | tf_op jit(solution)/shard_map/ppermute | solution.py:28
  111.1 2.6 collective-permute-start.14
  112.4 4.0 collective-permute-start.15
  204.1 2.6 collective-permute-start.16
  205.3 5.6 %collective-permute-start.17 = (f32[8,127]{1,0:T(8,128)S(1)}, f32[8,127]{1,0:T(8,128)S(1)}, u32[]{:S(2)}, u32[]{:S(2)}) collective-permute-start(f32[8,127]{1,0:T(8,128)S(1)} %get-tuple-element.151), channel_id=1, source_target_pairs={{1,0},{2,1},{3,2},{4,3},{5,4},{6,5},{7,6},{8,7},{9,8},{10,9},{11,1... | collective-permute-start | bytes 12200 | tf_op jit(solution)/shard_map/ppermute | solution.py:20
  211.2 56.8 %copy-start.7 = (s32[2]{0:T(128)S(1)}, s32[2]{0:T(128)}, u32[]{:S(2)}) copy-start(s32[2]{0:T(128)} %constant.175.clone.1) | copy-start | bytes 28
  213.5 6.2 %collective-permute-start.19 = (f32[8,128]{1,0:T(8,128)S(1)}, f32[8,128]{1,0:T(8,128)S(1)}, u32[]{:S(2)}, u32[]{:S(2)}) collective-permute-start(f32[8,128]{1,0:T(8,128)S(1)} %fusion.59), channel_id=1, source_target_pairs={{1,0},{2,1},{3,2},{4,3},{5,4},{6,5},{7,6},{8,7},{9,8},{10,9},{11,1... | collective-permute-start | bytes 12296 | tf_op jit(solution)/shard_map/ppermute | solution.py:28
  214.8 5.7 %collective-permute-start.18 = (f32[8,128]{1,0:T(8,128)S(1)}, f32[8,128]{1,0:T(8,128)S(1)}, u32[]{:S(2)}, u32[]{:S(2)}) collective-permute-start(f32[8,128]{1,0:T(8,128)S(1)} %fusion.59), channel_id=1, source_target_pairs={{0,1},{1,2},{2,3},{3,4},{4,5},{5,6},{6,7},{7,8},{8,9},{9,10},{10,1... | collective-permute-start | bytes 12296 | tf_op jit(solution)/shard_map/ppermute | solution.py:28
  220.5 7.7 %collective-permute-start.21 = (f32[8,128]{1,0:T(8,128)S(1)}, f32[8,128]{1,0:T(8,128)S(1)}, u32[]{:S(2)}, u32[]{:S(2)}) collective-permute-start(f32[8,128]{1,0:T(8,128)S(1)} %bitcast_add_fusion.26), channel_id=1, source_target_pairs={{2,0},{3,1},{4,2},{5,3},{6,4},{7,5},{8,6},{9,7},{10,8},{11,9},{12,... | collective-permute-start | bytes 12296 | tf_op jit(solution)/shard_map/ppermute | solution.py:28
  221.8 7.7 %collective-permute-start.20 = (f32[8,128]{1,0:T(8,128)S(1)}, f32[8,128]{1,0:T(8,128)S(1)}, u32[]{:S(2)}, u32[]{:S(2)}) collective-permute-start(f32[8,128]{1,0:T(8,128)S(1)} %bitcast_add_fusion.26), channel_id=1, source_target_pairs={{0,2},{1,3},{2,4},{3,5},{4,6},{5,7},{6,8},{7,9},{8,10},{9,11},{10,... | collective-permute-start | bytes 12296 | tf_op jit(solution)/shard_map/ppermute | solution.py:28
  229.5 9.9 %collective-permute-start.23 = (f32[8,128]{1,0:T(8,128)S(1)}, f32[8,128]{1,0:T(8,128)S(1)}, u32[]{:S(2)}, u32[]{:S(2)}) collective-permute-start(f32[8,128]{1,0:T(8,128)S(1)} %bitcast_add_fusion.24), channel_id=1, source_target_pairs={{4,0},{5,1},{6,2},{7,3},{8,4},{9,5},{10,6},{11,7},{12,8},{13,9},{1... | collective-permute-start | bytes 12296 | tf_op jit(solution)/shard_map/ppermute | solution.py:28
  230.8 9.9 %collective-permute-start.22 = (f32[8,128]{1,0:T(8,128)S(1)}, f32[8,128]{1,0:T(8,128)S(1)}, u32[]{:S(2)}, u32[]{:S(2)}) collective-permute-start(f32[8,128]{1,0:T(8,128)S(1)} %bitcast_add_fusion.24), channel_id=1, source_target_pairs={{0,4},{1,5},{2,6},{3,7},{4,8},{5,9},{6,10},{7,11},{8,12},{9,13},{1... | collective-permute-start | bytes 12296 | tf_op jit(solution)/shard_map/ppermute | solution.py:28
  240.8 9.6 %collective-permute-start.24 = (f32[8,128]{1,0:T(8,128)S(1)}, f32[8,128]{1,0:T(8,128)S(1)}, u32[]{:S(2)}, u32[]{:S(2)}) collective-permute-start(f32[8,128]{1,0:T(8,128)S(1)} %bitcast_add_fusion.22), channel_id=1, source_target_pairs={{0,8},{1,9},{2,10},{3,11},{4,12},{5,13},{6,14},{7,15},{8,16},{9,17... | collective-permute-start | bytes 12296 | tf_op jit(solution)/shard_map/ppermute | solution.py:28
  249.1 5.5 %collective-permute-start.25 = (f32[8,128]{1,0:T(8,128)S(1)}, f32[8,128]{1,0:T(8,128)S(1)}, u32[]{:S(2)}, u32[]{:S(2)}) collective-permute-start(f32[8,128]{1,0:T(8,128)S(1)} %bitcast_add_fusion.22), channel_id=1, source_target_pairs={{8,0},{9,1},{10,2},{11,3},{12,4},{13,5},{14,6},{15,7},{16,8},{17,9... | collective-permute-start | bytes 12296 | tf_op jit(solution)/shard_map/ppermute | solution.py:28
  254.6 6.8 %collective-permute-start.27 = (f32[8,128]{1,0:T(8,128)S(1)}, f32[8,128]{1,0:T(8,128)S(1)}, u32[]{:S(2)}, u32[]{:S(2)}) collective-permute-start(f32[8,128]{1,0:T(8,128)S(1)} %bitcast_add_fusion.20), channel_id=1, source_target_pairs={{16,0},{17,1},{18,2},{19,3},{20,4},{21,5},{22,6},{23,7},{24,8},{25... | collective-permute-start | bytes 12296 | tf_op jit(solution)/shard_map/ppermute | solution.py:28
  255.9 6.8 %collective-permute-start.26 = (f32[8,128]{1,0:T(8,128)S(1)}, f32[8,128]{1,0:T(8,128)S(1)}, u32[]{:S(2)}, u32[]{:S(2)}) collective-permute-start(f32[8,128]{1,0:T(8,128)S(1)} %bitcast_add_fusion.20), channel_id=1, source_target_pairs={{0,16},{1,17},{2,18},{3,19},{4,20},{5,21},{6,22},{7,23},{8,24},{9,... | collective-permute-start | bytes 12296 | tf_op jit(solution)/shard_map/ppermute | solution.py:28
  262.8 2.6 collective-permute-start.28
  264.1 3.6 collective-permute-start.29
  354.4 3.2 collective-permute-start.30
  355.7 5.6 %collective-permute-start.31 = (f32[8,127]{1,0:T(8,128)S(1)}, f32[8,127]{1,0:T(8,128)S(1)}, u32[]{:S(2)}, u32[]{:S(2)}) collective-permute-start(f32[8,127]{1,0:T(8,128)S(1)} %get-tuple-element.145), channel_id=1, source_target_pairs={{1,0},{2,1},{3,2},{4,3},{5,4},{6,5},{7,6},{8,7},{9,8},{10,9},{11,1... | collective-permute-start | bytes 12200 | tf_op jit(solution)/shard_map/ppermute | solution.py:20
  363.7 6.2 %collective-permute-start.33 = (f32[8,128]{1,0:T(8,128)S(1)}, f32[8,128]{1,0:T(8,128)S(1)}, u32[]{:S(2)}, u32[]{:S(2)}) collective-permute-start(f32[8,128]{1,0:T(8,128)S(1)} %fusion.56), channel_id=1, source_target_pairs={{1,0},{2,1},{3,2},{4,3},{5,4},{6,5},{7,6},{8,7},{9,8},{10,9},{11,1... | collective-permute-start | bytes 12296 | tf_op jit(solution)/shard_map/ppermute | solution.py:28
  365.0 5.7 %collective-permute-start.32 = (f32[8,128]{1,0:T(8,128)S(1)}, f32[8,128]{1,0:T(8,128)S(1)}, u32[]{:S(2)}, u32[]{:S(2)}) collective-permute-start(f32[8,128]{1,0:T(8,128)S(1)} %fusion.56), channel_id=1, source_target_pairs={{0,1},{1,2},{2,3},{3,4},{4,5},{5,6},{6,7},{7,8},{8,9},{9,10},{10,1... | collective-permute-start | bytes 12296 | tf_op jit(solution)/shard_map/ppermute | solution.py:28
  370.8 9.0 %collective-permute-start.35 = (f32[8,128]{1,0:T(8,128)S(1)}, f32[8,128]{1,0:T(8,128)S(1)}, u32[]{:S(2)}, u32[]{:S(2)}) collective-permute-start(f32[8,128]{1,0:T(8,128)S(1)} %bitcast_add_fusion.12), channel_id=1, source_target_pairs={{2,0},{3,1},{4,2},{5,3},{6,4},{7,5},{8,6},{9,7},{10,8},{11,9},{12,... | collective-permute-start | bytes 12296 | tf_op jit(solution)/shard_map/ppermute | solution.py:28
  373.4 7.7 %collective-permute-start.34 = (f32[8,128]{1,0:T(8,128)S(1)}, f32[8,128]{1,0:T(8,128)S(1)}, u32[]{:S(2)}, u32[]{:S(2)}) collective-permute-start(f32[8,128]{1,0:T(8,128)S(1)} %bitcast_add_fusion.12), channel_id=1, source_target_pairs={{0,2},{1,3},{2,4},{3,5},{4,6},{5,7},{6,8},{7,9},{8,10},{9,11},{10,... | collective-permute-start | bytes 12296 | tf_op jit(solution)/shard_map/ppermute | solution.py:28
  381.1 9.9 %collective-permute-start.37 = (f32[8,128]{1,0:T(8,128)S(1)}, f32[8,128]{1,0:T(8,128)S(1)}, u32[]{:S(2)}, u32[]{:S(2)}) collective-permute-start(f32[8,128]{1,0:T(8,128)S(1)} %bitcast_add_fusion.10), channel_id=1, source_target_pairs={{4,0},{5,1},{6,2},{7,3},{8,4},{9,5},{10,6},{11,7},{12,8},{13,9},{1... | collective-permute-start | bytes 12296 | tf_op jit(solution)/shard_map/ppermute | solution.py:28
  382.4 9.9 %collective-permute-start.36 = (f32[8,128]{1,0:T(8,128)S(1)}, f32[8,128]{1,0:T(8,128)S(1)}, u32[]{:S(2)}, u32[]{:S(2)}) collective-permute-start(f32[8,128]{1,0:T(8,128)S(1)} %bitcast_add_fusion.10), channel_id=1, source_target_pairs={{0,4},{1,5},{2,6},{3,7},{4,8},{5,9},{6,10},{7,11},{8,12},{9,13},{1... | collective-permute-start | bytes 12296 | tf_op jit(solution)/shard_map/ppermute | solution.py:28
  392.4 11.4 %collective-permute-start.38 = (f32[8,128]{1,0:T(8,128)S(1)}, f32[8,128]{1,0:T(8,128)S(1)}, u32[]{:S(2)}, u32[]{:S(2)}) collective-permute-start(f32[8,128]{1,0:T(8,128)S(1)} %bitcast_add_fusion.8), channel_id=1, source_target_pairs={{0,8},{1,9},{2,10},{3,11},{4,12},{5,13},{6,14},{7,15},{8,16},{9,17... | collective-permute-start | bytes 12296 | tf_op jit(solution)/shard_map/ppermute | solution.py:28
  402.6 5.5 %collective-permute-start.39 = (f32[8,128]{1,0:T(8,128)S(1)}, f32[8,128]{1,0:T(8,128)S(1)}, u32[]{:S(2)}, u32[]{:S(2)}) collective-permute-start(f32[8,128]{1,0:T(8,128)S(1)} %bitcast_add_fusion.8), channel_id=1, source_target_pairs={{8,0},{9,1},{10,2},{11,3},{12,4},{13,5},{14,6},{15,7},{16,8},{17,9... | collective-permute-start | bytes 12296 | tf_op jit(solution)/shard_map/ppermute | solution.py:28
  408.1 8.2 %collective-permute-start.41 = (f32[8,128]{1,0:T(8,128)S(1)}, f32[8,128]{1,0:T(8,128)S(1)}, u32[]{:S(2)}, u32[]{:S(2)}) collective-permute-start(f32[8,128]{1,0:T(8,128)S(1)} %bitcast_add_fusion.6), channel_id=1, source_target_pairs={{16,0},{17,1},{18,2},{19,3},{20,4},{21,5},{22,6},{23,7},{24,8},{25... | collective-permute-start | bytes 12296 | tf_op jit(solution)/shard_map/ppermute | solution.py:28
  410.8 6.8 %collective-permute-start.40 = (f32[8,128]{1,0:T(8,128)S(1)}, f32[8,128]{1,0:T(8,128)S(1)}, u32[]{:S(2)}, u32[]{:S(2)}) collective-permute-start(f32[8,128]{1,0:T(8,128)S(1)} %bitcast_add_fusion.6), channel_id=1, source_target_pairs={{0,16},{1,17},{2,18},{3,19},{4,20},{5,21},{6,22},{7,23},{8,24},{9,... | collective-permute-start | bytes 12296 | tf_op jit(solution)/shard_map/ppermute | solution.py:28
  417.7 2.6 collective-permute-start.42
  419.0 3.6 collective-permute-start.43
where the time goes:
time: 516 us; the launch traced here: 514 us
  blocking collectives  300 us (58%)
  starting transfers between devices  139 us (27%)
  waiting for transfers between devices  42.9 us (8%)
  other arithmetic  16.6 us (3%)
  local copies, waits for them, and re-layouts  8.92 us (2%)
  between operations  5.46 us (1%)
    psum x3, blocking collectives, on_device(): dots = lax.psum(local_dots, 'chain') / count  133 us
    psum x3, blocking collectives, on_device(): squares = lax.psum(jnp.sum(vector * vector), 'chain') / count  120 us
    ppermute x30, starting transfers between devices, from_behind(): return lax.ppermute(x, axis, pairs)  120 us
    psum x1, blocking collectives, on_device(): start_sum = lax.psum(jnp.sum(right_side * right_side), 'chain')  47.2 us
    ppermute x30, waiting for transfers between devices, from_behind(): return lax.ppermute(x, axis, pairs)  23.5 us
    ppermute x7, waiting for transfers between devices, padded_2(): after = lax.ppermute(initial, axis, down)  19.4 us
  transfers between devices with their start and end apart: 44, of which 21 were waited for; matrix products, arithmetic and copies ran while one was open for 1% of the time, Pallas kernels for 0%

commit v1 on v0

--- a/solution.py
+++ b/solution.py
@@ -1,12 +1,18 @@
+import functools
+
 import jax
 import jax.numpy as jnp
 from jax import lax
+from jax.experimental import pallas as pl
+from jax.experimental.pallas import tpu as pltpu
 from jax.sharding import PartitionSpec as P
 
 ITERS = 3
 
 
 EPS = 1e-06
+AXIS = "chain"
+SUB = 8
 
 
 def padded_2(x, sides, width):
@@ -32,7 +38,7 @@
     return jnp.einsum("abi,bi->ai", blocks, field, precision=lax.Precision.HIGHEST)
 
 
-def on_device(
+def general(
     right_side, diag_block, below_block, above_block, lower_level, upper_level, final_block
 ):
     rows_here = right_side.shape[1]
@@ -91,6 +97,422 @@
     return (jnp.stack(basis), hess)
 
 
+class Plan:
+    def __init__(self, devices, rows, depth):
+        self.devices, self.rows, self.depth = devices, rows, depth
+        self.piece = rows // devices
+        self.near = [k for k in range(depth) if 2**k < rows]
+        self.far = [k for k in range(depth) if rows <= 2**k < rows * devices]
+        self.sent = len(self.near) - 1
+        self.count = SUB * rows * devices
+        n = len(self.far)
+        self.own_mats = 2 * n + 4
+        self.halo_mats = 2 * n + 1
+        self.own_tiles = self.own_mats * SUB
+        self.halo_tiles = self.halo_mats * SUB
+        self.halo_packed = self.halo_tiles // 2
+        self.coef_tiles = self.own_tiles + self.halo_packed
+        self.per_group = rows // SUB
+        tiles = self.coef_tiles + 4
+        groups = -(-tiles // self.per_group)
+        step = max(1, SUB // self.piece)
+        self.groups = -(-groups // step) * step
+        self.chunk = self.groups * self.piece
+        self.width = rows // self.piece
+
+
+def fits(devices, rows, block, lanes=128):
+    piece = rows // devices
+    return block == SUB and rows == lanes and piece >= 1 and piece * devices == rows and rows // piece >= 4 * SUB
+
+
+def lane(shape=(SUB, 128)):
+    return lax.broadcasted_iota(jnp.int32, shape, 1)
+
+
+def sub(shape=(SUB, 128)):
+    return lax.broadcasted_iota(jnp.int32, shape, 0)
+
+
+def spread(v, b):
+    return jnp.broadcast_to(v[b : b + 1, :], v.shape)
+
+
+def total(x):
+    return jnp.sum(jnp.sum(x, axis=0, keepdims=True), axis=1, keepdims=True)
+
+
+def send(plan, tiles, z_ref, out_ref):
+    r = plan.rows
+    stacked = jnp.concatenate(tiles + [jnp.zeros((r - SUB * len(tiles), r), jnp.float32)], 0)
+    z_ref[...] = stacked.T
+    out = z_ref[pl.ds(0, plan.devices, stride=plan.piece), :]
+    for i in range(1, plan.piece):
+        part = z_ref[pl.ds(i, plan.devices, stride=plan.piece), :]
+        out = out + pltpu.roll(part, i * plan.width, 1)
+    out_ref[...] = out
+
+
+def receive(plan, in_ref, z_ref):
+    got = in_ref[...]
+    for i in range(plan.piece):
+        part = got if i == 0 else pltpu.roll(got, plan.rows - i * plan.width, 1)
+        z_ref[pl.ds(i, plan.devices, stride=plan.piece), :] = part
+    t = z_ref[...].T
+    return [t[SUB * k : SUB * k + SUB] for k in range(4)]
+
+
+def halo_of(plan, y):
+    pos = lane() % plan.piece
+    before, after = pltpu.roll(y, 1, 1), pltpu.roll(y, plan.rows - 1, 1)
+    return jnp.where(pos == 0, before, jnp.where(pos == plan.piece - 1, after, 0.0))
+
+
+def wrapped(plan, x):
+    q, r = plan.piece, plan.rows
+    me = lax.axis_index(AXIS)
+    at = lane()
+    pos = at % q
+    later = jnp.where(at == 0, 0.0, pltpu.roll(x, q, 1))
+    sooner = jnp.where(at == r - 1, 0.0, pltpu.roll(x, r - q, 1))
+    first = jnp.where(me == 0, later, x)
+    last = jnp.where(me == plan.devices - 1, sooner, x)
+    return jnp.where(pos == 0, first, jnp.where(pos == q - 1, last, 0.0))
+
+
+def near_levels(plan, v, lo_ref, up_ref, prev_ref, next_ref):
+    r = plan.rows
+    at = lane()
+    for k in plan.near:
+        s = 2**k
+        turned = [pltpu.roll(x, s, 1) for x in v]
+        back = [pltpu.roll(x, r - s, 1) for x in v]
+        lower = [turned[0]] + [jnp.where(at < s, turned[t - 1], turned[t]) for t in (1, 2)]
+        upper = [jnp.where(at >= r - s, back[t + 1], back[t]) for t in (0, 1)] + [back[2]]
+        fresh = list(v)
+        for t in (0, 1, 2) if k < plan.sent else (1,):
+            low_sum = high_sum = None
+            for b in range(SUB):
+                if t == 1:
+                    lc = lo_ref[pl.ds(64 * k + b, SUB, stride=SUB), :]
+                    uc = up_ref[pl.ds(64 * k + b, SUB, stride=SUB), :]
+                else:
+                    ref = prev_ref if t == 0 else next_ref
+                    lc = ref[pl.ds(64 * k + b, SUB, stride=SUB), :]
+                    uc = ref[pl.ds(64 * (plan.sent + k) + b, SUB, stride=SUB), :]
+                low = lc * spread(lower[t], b)
+                high = uc * spread(upper[t], b)
+                low_sum = low if low_sum is None else low_sum + low
+                high_sum = high if high_sum is None else high_sum + high
+            fresh[t] = v[t] + low_sum + high_sum
+        v = fresh
+    return v[1]
+
+
+def square_tile(u):
+    return jnp.where(sub() == 0, jnp.broadcast_to(total(u * u), u.shape), 0.0)
+
+
+def pack_kernel(plan, lo_ref, up_ref, rhs_ref, out_ref):
+    n = 64 * plan.sent
+    out_ref[pl.ds(0, n), :] = lo_ref[pl.ds(0, n), :]
+    out_ref[pl.ds(n, n), :] = up_ref[pl.ds(0, n), :]
+    out_ref[pl.ds(2 * n, SUB), :] = rhs_ref[...]
+
+
+def first_kernel(
+    plan, lo_ref, up_ref, fin_ref, dia_ref, bel_ref, abo_ref, rhs_ref, prev_ref, next_ref, out_ref, z_ref
+):
+    n = 64 * 2 * plan.sent
+    rhs = rhs_ref[...]
+    y = near_levels(
+        plan,
+        [prev_ref[pl.ds(n, SUB), :], rhs, next_ref[pl.ds(n, SUB), :]],
+        lo_ref,
+        up_ref,
+        prev_ref,
+        next_ref,
+    )
+    mats = [(lo_ref, 64 * k) for k in plan.far] + [(up_ref, 64 * k) for k in plan.far]
+    mats += [(fin_ref, 0), (dia_ref, 0), (bel_ref, 0), (abo_ref, 0)]
+
+    def raw(index):
+        ref, base = mats[index // SUB]
+        return ref[pl.ds(base + index % SUB, SUB, stride=SUB), :]
+
+    def tile(index):
+        if index < plan.own_tiles:
+            return raw(index)
+        if index < plan.coef_tiles:
+            j = 2 * (index - plan.own_tiles)
+            a, b = halo_of(plan, raw(j)), halo_of(plan, raw(j + 1))
+            pos = lane() % plan.piece
+            moved = jnp.where(pos == 1, pltpu.roll(b, 1, 1), pltpu.roll(b, plan.rows - 1, 1))
+            return jnp.where((pos == 0) | (pos == plan.piece - 1), a, moved)
+        extra = index - plan.coef_tiles
+        if extra == 0:
+            return y
+        if extra == 1:
+            return halo_of(plan, y)
+        if extra == 2:
+            return square_tile(rhs)
+        if extra == 3:
+            return rhs
+        return jnp.zeros((SUB, plan.rows), jnp.float32)
+
+    g_tiles = plan.per_group
+    for g in range(plan.groups):
+        block = jnp.concatenate([tile(g * g_tiles + t) for t in range(g_tiles)], 0)
+        z_ref[g] = block.T
+        for i in range(plan.piece):
+            out_ref[pl.ds(g * plan.piece + i, plan.devices, stride=plan.chunk), :] = z_ref[
+                g, pl.ds(i, plan.devices, stride=plan.piece), :
+            ]
+
+
+def far_stage(plan, own, halo, coef_ref):
+    q, r, n = plan.piece, plan.rows, len(plan.far)
+    base = plan.own_tiles
+
+    def apply(mat, x, start):
+        out = coef_ref[start + mat * SUB] * spread(x, 0)
+        for b in range(1, SUB):
+            out = out + coef_ref[start + mat * SUB + b] * spread(x, b)
+        return out
+
+    for k in range(n):
+        by = q * 2**k
+        fresh = []
+        for x, start in ((own, 0), (halo, base)):
+            low = apply(k, pltpu.roll(x, by, 1), start)
+            high = apply(n + k, pltpu.roll(x, r - by, 1), start)
+            fresh.append(x + low + high)
+        own, halo = fresh
+    own = own + apply(2 * n, own, 0)
+    halo = wrapped(plan, halo + apply(2 * n, halo, base))
+    pos = lane() % q
+    before = jnp.where(pos == 0, halo, pltpu.roll(own, 1, 1))
+    after = jnp.where(pos == q - 1, halo, pltpu.roll(own, r - 1, 1))
+    w = 2.0 * own + apply(2 * n + 1, own, 0)
+    return w + apply(2 * n + 2, before, 0) + apply(2 * n + 3, after, 0)
+
+
+def norm_of(plan, squares):
+    pos = lane() % plan.piece
+    one = jnp.where((pos == 0) & (sub() == 0), squares, 0.0)
+    return jnp.sqrt(jnp.broadcast_to(total(one), one.shape) / plan.count + EPS)
+
+
+def finish_far(plan, y, halo, s, vs, coef_ref, z_ref, out_ref):
+    w = far_stage(plan, y / s, halo / s, coef_ref)
+    q, r = plan.piece, plan.rows
+    at = lane()
+    before = jnp.where(at < q, 0.0, pltpu.roll(w, q, 1))
+    after = jnp.where(at >= r - q, 0.0, pltpu.roll(w, r - q, 1))
+    dots = jnp.zeros_like(w)
+    for i, v in enumerate(vs):
+        dots = jnp.where(sub() == i, jnp.broadcast_to(total(v * w), w.shape), dots)
+    send(plan, [before, w, after, dots], z_ref, out_ref)
+    return w
+
+
+def start_far_kernel(plan, in_ref, out_ref, coef_ref, w_ref, v_ref, s_ref, z_ref, zs_ref):
+    q, r = plan.piece, plan.rows
+    at = lane()
+    pos = at % q
+    n = len(plan.far)
+    g_tiles = plan.per_group
+    extra = []
+    for g in range(plan.groups):
+        for i in range(q):
+            z_ref[g, pl.ds(i, plan.devices, stride=q), :] = in_ref[
+                pl.ds(g * q + i, plan.devices, stride=plan.chunk), :
+            ]
+        t = z_ref[g].T
+        for j in range(g_tiles):
+            index = g * g_tiles + j
+            tile = t[SUB * j : SUB * j + SUB]
+
+            def limited(x, mat):
+                if mat < n:
+                    return jnp.where(at < q * 2**mat, 0.0, x)
+                if mat < 2 * n:
+                    return jnp.where(at >= r - q * 2 ** (mat - n), 0.0, x)
+                return x
+
+            if index < plan.own_tiles:
+                coef_ref[index] = limited(tile, index // SUB)
+            elif index < plan.coef_tiles:
+                k = 2 * (index - plan.own_tiles)
+                other = jnp.where(pos == 0, pltpu.roll(tile, r - 1, 1), pltpu.roll(tile, 1, 1))
+                coef_ref[plan.own_tiles + k] = limited(tile, k // SUB)
+                coef_ref[plan.own_tiles + k + 1] = limited(other, (k + 1) // SUB)
+            elif index < plan.coef_tiles + 4:
+                extra.append(tile)
+    y, halo, squares, rhs = extra
+    s = norm_of(plan, squares)
+    v = rhs / s
+    v_ref[...] = v
+    s_ref[...] = s
+    w_ref[...] = finish_far(plan, y, halo, s, [v], coef_ref, zs_ref, out_ref)
+
+
+def near_kernel(plan, j, in_ref, lo_ref, up_ref, rhs_ref, prev_ref, next_ref, *rest):
+    us, ss = rest[: j - 1], rest[j - 1 : 2 * j - 1]
+    out_ref, u_ref, h_ref, zr_ref, zs_ref = rest[2 * j - 1 :]
+    n = 64 * 2 * plan.sent
+    prev, own, nxt, dots = receive(plan, in_ref, zr_ref)
+    pos = lane() % plan.piece
+    h = jnp.sum(jnp.where(pos == 0, dots, 0.0), axis=1, keepdims=True) / plan.count
+    h = jnp.broadcast_to(h, dots.shape)
+    h_ref[...] = h
+    w = [prev, own, nxt]
+    fields = [[prev_ref[pl.ds(n, SUB), :], rhs_ref[...], next_ref[pl.ds(n, SUB), :]]]
+    fields += [[u[t] for t in range(3)] for u in us]
+    for t in range(3):
+        acc = None
+        for i in range(j):
+            term = spread(h, i) * (fields[i][t] / ss[i][...])
+            acc = term if acc is None else acc + term
+        w[t] = w[t] - acc
+        u_ref[t] = w[t]
+    y = near_levels(plan, w, lo_ref, up_ref, prev_ref, next_ref)
+    send(plan, [y, halo_of(plan, y), square_tile(w[1])], zs_ref, out_ref)
+
+
+def far_kernel(plan, j, in_ref, coef_ref, h_ref, w_in_ref, *rest):
+    vs = [v[...] for v in rest[:j]]
+    out_ref, w_ref, v_ref, s_ref, zr_ref, zs_ref = rest[j:]
+    y, halo, squares, _ = receive(plan, in_ref, zr_ref)
+    s = norm_of(plan, squares)
+    h = h_ref[...]
+    acc = None
+    for i in range(j):
+        term = spread(h, i) * vs[i]
+        acc = term if acc is None else acc + term
+    v = (w_in_ref[...] - acc) / s
+    v_ref[...] = v
+    s_ref[...] = s
+    w_ref[...] = finish_far(plan, y, halo, s, vs + [v], coef_ref, zs_ref, out_ref)
+
+
+def last_kernel(plan, in_ref, rhs_ref, *rest):
+    us, ss = rest[: ITERS - 1], rest[ITERS - 1 : 2 * ITERS - 1]
+    u_ref, h_ref, out_ref, zr_ref = rest[2 * ITERS - 1 :]
+    _, own, _, dots = receive(plan, in_ref, zr_ref)
+    pos = lane() % plan.piece
+    h = jnp.sum(jnp.where(pos == 0, dots, 0.0), axis=1, keepdims=True) / plan.count
+    h = jnp.broadcast_to(h, dots.shape)
+    h_ref[...] = h
+    fields = [rhs_ref[...]] + [u[1] for u in us]
+    acc = None
+    for i in range(ITERS):
+        term = spread(h, i) * (fields[i] / ss[i][...])
+        acc = term if acc is None else acc + term
+    u = own - acc
+    u_ref[...] = u
+    out_ref[...] = jnp.broadcast_to(total(u * u), out_ref.shape)
+
+
+def output_kernel(plan, in_ref, rhs_ref, *rest):
+    us = [u[1] for u in rest[: ITERS - 1]] + [rest[ITERS - 1][...]]
+    ss = [s[...] for s in rest[ITERS : 2 * ITERS]]
+    hs = [h[...] for h in rest[2 * ITERS : 3 * ITERS]]
+    basis_ref, hess_ref = rest[3 * ITERS :]
+    squares = jnp.sum(in_ref[...], axis=0, keepdims=True)
+    ss.append(jnp.broadcast_to(jnp.sqrt(squares / plan.count + EPS), ss[0].shape))
+    fields = [rhs_ref[...]] + us
+    for j in range(ITERS + 1):
+        basis_ref[j] = fields[j] / ss[j]
+    hess = jnp.zeros_like(ss[0])
+    for j in range(ITERS):
+        col = jnp.where(sub() <= j, hs[j], jnp.where(sub() == j + 1, ss[j + 1], 0.0))
+        hess = jnp.where(lane() == j, col, hess)
+    hess_ref[...] = hess[: ITERS + 1, :ITERS]
+
+
+def transposed(
+    plan, right_side, diag_block, below_block, above_block, lower_level, upper_level, final_block
+):
+    r, d = plan.rows, plan.devices
+    flat = lambda x: x.reshape(-1, r)
+    lo, up, fin = flat(lower_level), flat(upper_level), flat(final_block)
+    dia, bel, abo = flat(diag_block), flat(below_block), flat(above_block)
+    shape = lambda *s: jax.ShapeDtypeStruct(s, jnp.float32)
+    tile = shape(SUB, r)
+    scratch = lambda *s: pltpu.VMEM(s, jnp.float32)
+
+    def call(kernel, outs, scratches, *args):
+        return pl.pallas_call(
+            kernel,
+            out_shape=outs,
+            in_specs=[pl.BlockSpec(memory_space=pltpu.VMEM)] * len(args),
+            out_specs=jax.tree.map(lambda _: pl.BlockSpec(memory_space=pltpu.VMEM), outs),
+            scratch_shapes=scratches,
+            compiler_params=pltpu.CompilerParams(vmem_limit_bytes=24 * 2**20),
+            cost_estimate=pl.CostEstimate(flops=4_000_000, bytes_accessed=2_000_000, transcendentals=0),
+        )(*args)
+
+    def exchange(x):
+        y = lax.all_to_all(x.reshape(d, -1, r), AXIS, 0, 0)
+        return y.reshape(-1, r)
+
+    part = functools.partial
+    edge = call(part(pack_kernel, plan), shape(64 * 2 * plan.sent + SUB, r), [], lo, up, right_side)
+    prev = lax.ppermute(edge, AXIS, [(i, i + 1) for i in range(d - 1)])
+    nxt = lax.ppermute(edge, AXIS, [(i + 1, i) for i in range(d - 1)])
+    big = call(
+        part(first_kernel, plan),
+        shape(d * plan.chunk, r),
+        [scratch(plan.groups, r, r)],
+        lo, up, fin, dia, bel, abo, right_side, prev, nxt,
+    )
+    got = exchange(big)
+    small = shape(d, r)
+    out, coef, w, v, s = call(
+        part(start_far_kernel, plan),
+        (small, shape(plan.own_tiles + plan.halo_tiles, SUB, r), tile, tile, tile),
+        [scratch(plan.groups, r, r), scratch(r, r)],
+        got,
+    )
+    us, ss, vs, hs = [], [s], [v], []
+    for j in range(1, ITERS):
+        out, u, h = call(
+            part(near_kernel, plan, j),
+            (small, shape(3, SUB, r), tile),
+            [scratch(r, r), scratch(r, r)],
+            exchange(out), lo, up, right_side, prev, nxt, *us, *ss,
+        )
+        us.append(u)
+        hs.append(h)
+        out, w, v, s = call(
+            part(far_kernel, plan, j),
+            (small, tile, tile, tile),
+            [scratch(r, r), scratch(r, r)],
+            exchange(out), coef, h, w, *vs,
+        )
+        vs.append(v)
+        ss.append(s)
+    u, h, out = call(
+        part(last_kernel, plan), (tile, tile, small), [scratch(r, r)], exchange(out), right_side, *us, *ss
+    )
+    hs.append(h)
+    return call(
+        part(output_kernel, plan),
+        (shape(ITERS + 1, SUB, r), shape(ITERS + 1, ITERS)),
+        [],
+        exchange(out), right_side, *us, u, *ss, *hs,
+    )
+
+
+def on_device(*args):
+    right_side, lower_level = args[0], args[4]
+    devices, rows = lax.axis_size(AXIS), right_side.shape[1]
+    if not fits(devices, rows, right_side.shape[0]):
+        return general(*args)
+    return tuple(transposed(Plan(devices, rows, lower_level.shape[0]), *args))
+
+
 def solution(mesh):
     return jax.shard_map(
         on_device,

time: 516 us -> 107 us (0.21)
  blocking collectives: 300 us -> 87.6 us
  starting transfers between devices: 139 us -> 4.48 us
  waiting for transfers between devices: 42.9 us -> 1.3 us
  other arithmetic: 16.6 us -> 0 us
  Pallas kernels: 0 us -> 9.69 us
  local copies, waits for them, and re-layouts: 8.92 us -> 2.7 us
    psum x7 -> x0, blocking collectives: 300 us -> none  [the longest x3 133 us: on_device(): dots = lax.psum(local_dots, 'chain') / count]
    ppermute x44 -> x2, starting transfers between devices: 139 us -> 4.48 us  [the longest x1 3.06 us: transposed(): prev = lax.ppermute(edge, AXIS, [(i, i + 1) for i in range(d - 1)])]
    all_to_all x0 -> x7, blocking collectives: none -> 87.6 us  [exchange(): y = lax.all_to_all(x.reshape(d, -1, r), AXIS, 0, 0)]
    ppermute x44 -> x2, waiting for transfers between devices: 42.9 us -> 1.3 us  [the longest x1 1.3 us: transposed(): prev = lax.ppermute(edge, AXIS, [(i, i + 1) for i in range(d - 1)])]
    pallas_call x0 -> x9, Pallas kernels: none -> 9.69 us  [call(): pl.pallas_call(kernel, out_shape=outs, in_specs=[pl.BlockSpec(memory_spac...]
    another operation x11 -> x0, other arithmetic: 5.91 us -> none
    dot_general x84 -> x0, other arithmetic: 5.32 us -> none  [the longest x83 4.72 us: blockmul(): jnp.einsum('abi,bi->ai', blocks, field, precision=lax.Precision.HIGHEST)]
  transfers between devices with their start and end apart: 44 -> 2, of which waited for: 21 -> 1; matrix products, arithmetic and copies ran while one was open for 1% -> 0% of each run, Pallas kernels for 0% -> 0%
where the time goes in v1:
time: 107 us; the launch traced here: 106 us
  blocking collectives  87.6 us (82%)
  Pallas kernels  9.69 us (9%)
  starting transfers between devices  4.48 us (4%)
  local copies, waits for them, and re-layouts  2.7 us (3%)
  waiting for transfers between devices  1.3 us (1%)
    all_to_all x7, blocking collectives, exchange(): y = lax.all_to_all(x.reshape(d, -1, r), AXIS, 0, 0)  87.6 us
    pallas_call x9, Pallas kernels, call(): pl.pallas_call(kernel, out_shape=outs, in_specs=[pl.BlockSpec(memory_spac...  9.69 us
    ppermute x1, starting transfers between devices, transposed(): prev = lax.ppermute(edge, AXIS, [(i, i + 1) for i in range(d - 1)])  3.06 us
    unnamed x18, local copies, waits for them, and re-layouts  2.7 us
  transfers between devices with their start and end apart: 2, of which 1 were waited for; matrix products, arithmetic and copies ran while one was open for 0% of the time, Pallas kernels for 0%

profile of v1, /device:TPU:0, one launch (start us, length us, event | category | flops | bytes accessed | tf_op | source)
XLA Modules:
  0.0 106.5 jit_solution(5751942055540399508)
XLA Ops:
  0.6 0.0 copy-start
  0.6 1.0 copy-done
  1.6 0.0 copy-start.2
  1.6 1.0 copy-done.2
  2.6 0.0 copy-start.4
  2.6 0.7 copy-done.4
  3.3 0.0 copy-start.5
  3.3 0.0 copy-start.6
  3.3 0.0 copy-start.7
  3.3 0.0 copy-start.8
  3.4 1.4 %collective-permute-start.1 = (f32[776,128]{1,0:T(8,128)S(1)}, f32[776,128]{1,0:T(8,128)S(1)}, u32[]{:S(2)}, u32[]{:S(2)}) collective-permute-start(f32[776,128]{1,0:T(8,128)S(1)} %shard_map.86), channel_id=1, source_target_pairs={{1,0},{2,1},{3,2},{4,3},{5,4},{6,5},{7,6},{8,7},{9,8},{10,9},{11,1... | collective-permute-start | bytes 1191944 | tf_op jit(solution)/shard_map/ppermute | solution.py:463
  4.8 3.1 %collective-permute-start = (f32[776,128]{1,0:T(8,128)S(1)}, f32[776,128]{1,0:T(8,128)S(1)}, u32[]{:S(2)}, u32[]{:S(2)}) collective-permute-start(f32[776,128]{1,0:T(8,128)S(1)} %shard_map.86), channel_id=1, source_target_pairs={{0,1},{1,2},{2,3},{3,4},{4,5},{5,6},{6,7},{7,8},{8,9},{9,10},{10,1... | collective-permute-start | bytes 1191944 | tf_op jit(solution)/shard_map/ppermute | solution.py:462
  7.9 0.0 collective-permute-done.1.next_ref
  7.9 1.3 %collective-permute-done.prev_ref = f32[776,128]{1,0:T(8,128)S(1)} collective-permute-done((f32[776,128]{1,0:T(8,128)S(1)}, f32[776,128]{1,0:T(8,128)S(1)}, u32[]{:S(2)}, u32[]{:S(2)}) %collective-permute-start) | collective-permute-done | bytes 397344 | tf_op jit(solution)/shard_map/ppermute | solution.py:462
  9.2 0.0 copy-done.5
  9.2 0.0 copy-done.6
  9.2 0.0 copy-done.7
  9.2 0.0 copy-done.8
  9.2 3.1 %shard_map.87 = f32[1280,128]{1,0:T(8,128)S(1)} custom-call(f32[768,128]{1,0:T(8,128)S(1)} %bitcast.33, f32[768,128]{1,0:T(8,128)S(1)} %bitcast.37, f32[64,128]{1,0:T(8,128)S(1)} %bitcast.48, f32[64,128]{1,0:T(8,128)S(1)} %bitcast.49, f32[64,128]{1,0:T(8,128)S(1)} %bitcast.50, f32[64,128]{1,0:T(8,128)S(1)} %bitcast.51, f32[8,128]{1,0:T(8,128)S(1)} %copy-done.4, ...), custom_call_target="tpu_custom_call" | custom-call | flops 4000000 | bytes 2000000 | tf_op jit(solution)/shard_map/pallas_call | solution.py:446
  12.3 0.0 copy-start.3
  12.3 32.8 %all_to_all.35 = f32[32,40,128]{2,1,0:T(8,128)S(1)} all-to-all(f32[32,40,128]{2,1,0:T(8,128)S(1)} %bitcast.40), channel_id=1, replica_groups=mesh['chain'=32] {'chain'}, dimensions={0} | all-to-all | bytes 1310720 | tf_op jit(solution)/shard_map/all_to_all | solution.py:457
  45.1 0.0 copy-start.1
  45.1 1.1 %shard_map.88 = (f32[32,128]{1,0:T(8,128)S(1)}, f32[200,8,128]{2,1,0:T(8,128)S(1)}, f32[8,128]{1,0:T(8,128)S(1)}, f32[8,128]{1,0:T(8,128)S(1)}, f32[8,128]{1,0:T(8,128)S(1)}) custom-call(f32[1280,128]{1,0:T(8,128)S(1)} %bitcast.41), custom_call_target="tpu_custom_call" | custom-call | flops 4000000 | bytes 2000000 | tf_op jit(solution)/shard_map/pallas_call | solution.py:446
  46.2 10.4 %all_to_all.36 = f32[32,1,128]{2,1,0:T(1,128)S(1)} all-to-all(f32[32,1,128]{2,1,0:T(1,128)S(1)} %bitcast.53), channel_id=1, replica_groups=mesh['chain'=32] {'chain'}, dimensions={0} | all-to-all | bytes 32768 | tf_op jit(solution)/shard_map/all_to_all | solution.py:457
  56.6 0.0 copy-done.3
  56.6 0.0 copy-done.1
  56.6 1.1 %shard_map.89 = (f32[32,128]{1,0:T(8,128)S(1)}, f32[3,8,128]{2,1,0:T(8,128)S(1)}, f32[8,128]{1,0:T(8,128)S(1)}) custom-call(f32[32,128]{1,0:T(8,128)S(1)} %bitcast.43, f32[768,128]{1,0:T(8,128)S(1)} %bitcast.34, f32[768,128]{1,0:T(8,128)S(1)} %bitcast.38, f32[8,128]{1,0:T(8,128)S(1)} %copy-done.4, f32[776,128]{1,0:T(8,128)S(1)} %collective-permute-done.prev_ref, ...), custom_call_target="tpu_custom_call" | custom-call | flops 4000000 | bytes 2000000 | tf_op jit(solution)/shard_map/pallas_call | solution.py:446
  57.7 8.9 %all_to_all.37 = f32[32,1,128]{2,1,0:T(1,128)S(1)} all-to-all(f32[32,1,128]{2,1,0:T(1,128)S(1)} %bitcast.56), channel_id=1, replica_groups=mesh['chain'=32] {'chain'}, dimensions={0} | all-to-all | bytes 32768 | tf_op jit(solution)/shard_map/all_to_all | solution.py:457
  66.6 1.0 shard_map.90
  67.6 8.9 %all_to_all.38 = f32[32,1,128]{2,1,0:T(1,128)S(1)} all-to-all(f32[32,1,128]{2,1,0:T(1,128)S(1)} %bitcast.54), channel_id=1, replica_groups=mesh['chain'=32] {'chain'}, dimensions={0} | all-to-all | bytes 32768 | tf_op jit(solution)/shard_map/all_to_all | solution.py:457
  76.5 1.1 %shard_map.91 = (f32[32,128]{1,0:T(8,128)S(1)}, f32[3,8,128]{2,1,0:T(8,128)S(1)}, f32[8,128]{1,0:T(8,128)S(1)}) custom-call(f32[32,128]{1,0:T(8,128)S(1)} %bitcast.42, f32[768,128]{1,0:T(8,128)S(1)} %bitcast.35, f32[768,128]{1,0:T(8,128)S(1)} %bitcast.39, f32[8,128]{1,0:T(8,128)S(1)} %copy-done.4, f32[776,128]{1,0:T(8,128)S(1)} %collective-permute-done.prev_ref, ...), custom_call_target="tpu_custom_call" | custom-call | flops 4000000 | bytes 2000000 | tf_op jit(solution)/shard_map/pallas_call | solution.py:446
  77.6 8.9 %all_to_all.39 = f32[32,1,128]{2,1,0:T(1,128)S(1)} all-to-all(f32[32,1,128]{2,1,0:T(1,128)S(1)} %bitcast.55), channel_id=1, replica_groups=mesh['chain'=32] {'chain'}, dimensions={0} | all-to-all | bytes 32768 | tf_op jit(solution)/shard_map/all_to_all | solution.py:457
  86.5 1.4 %shard_map.92 = (f32[32,128]{1,0:T(8,128)S(1)}, f32[8,128]{1,0:T(8,128)}, f32[8,128]{1,0:T(8,128)}, f32[8,128]{1,0:T(8,128)S(1)}) custom-call(f32[32,128]{1,0:T(8,128)S(1)} %bitcast.47, f32[200,8,128]{2,1,0:T(8,128)S(1)} %get-tuple-element.25.coef_ref, f32[8,128]{1,0:T(8,128)S(1)} %get-tuple-element.33.h_ref.rest_7_, ...), custom_call_target="tpu_custom_call" | custom-call | flops 4000000 | bytes 2000000 | tf_op jit(solution)/shard_map/pallas_call | solution.py:446
  87.8 8.9 %all_to_all.40 = f32[32,1,128]{2,1,0:T(1,128)S(1)} all-to-all(f32[32,1,128]{2,1,0:T(1,128)S(1)} %bitcast.52), channel_id=1, replica_groups=mesh['chain'=32] {'chain'}, dimensions={0} | all-to-all | bytes 32768 | tf_op jit(solution)/shard_map/all_to_all | solution.py:457
  96.7 0.3 shard_map.93
  96.9 8.9 %all_to_all.41 = f32[32,1,128]{2,1,0:T(1,128)S(1)} all-to-all(f32[32,1,128]{2,1,0:T(1,128)S(1)} %bitcast.57), channel_id=1, replica_groups=mesh['chain'=32] {'chain'}, dimensions={0} | all-to-all | bytes 32768 | tf_op jit(solution)/shard_map/all_to_all | solution.py:457
  105.9 0.6 shard_map.94
  (1 shorter events, 0.0 us)
Async XLA Ops:
  0.6 1.0 copy-start
  1.6 1.0 copy-start.2
  2.6 0.7 copy-start.4
  3.3 5.9 %copy-start.5 = (f32[8,8,128]{2,1,0:T(8,128)S(1)}, f32[8,8,128]{2,1,0:T(8,128)}, u32[]{:S(2)}) copy-start(f32[8,8,128]{2,1,0:T(8,128)} %param.13) | copy-start | bytes 98308
  3.3 5.9 %copy-start.6 = (f32[8,8,128]{2,1,0:T(8,128)S(1)}, f32[8,8,128]{2,1,0:T(8,128)}, u32[]{:S(2)}) copy-start(f32[8,8,128]{2,1,0:T(8,128)} %param.8) | copy-start | bytes 98308
  3.3 5.9 %copy-start.7 = (f32[8,8,128]{2,1,0:T(8,128)S(1)}, f32[8,8,128]{2,1,0:T(8,128)}, u32[]{:S(2)}) copy-start(f32[8,8,128]{2,1,0:T(8,128)} %param.9) | copy-start | bytes 98308
  3.3 5.9 %copy-start.8 = (f32[8,8,128]{2,1,0:T(8,128)S(1)}, f32[8,8,128]{2,1,0:T(8,128)}, u32[]{:S(2)}) copy-start(f32[8,8,128]{2,1,0:T(8,128)} %param.10) | copy-start | bytes 98308
  3.4 4.5 %collective-permute-start.1 = (f32[776,128]{1,0:T(8,128)S(1)}, f32[776,128]{1,0:T(8,128)S(1)}, u32[]{:S(2)}, u32[]{:S(2)}) collective-permute-start(f32[776,128]{1,0:T(8,128)S(1)} %shard_map.86), channel_id=1, source_target_pairs={{1,0},{2,1},{3,2},{4,3},{5,4},{6,5},{7,6},{8,7},{9,8},{10,9},{11,1... | collective-permute-start | bytes 1191944 | tf_op jit(solution)/shard_map/ppermute | solution.py:463
  4.8 4.4 %collective-permute-start = (f32[776,128]{1,0:T(8,128)S(1)}, f32[776,128]{1,0:T(8,128)S(1)}, u32[]{:S(2)}, u32[]{:S(2)}) collective-permute-start(f32[776,128]{1,0:T(8,128)S(1)} %shard_map.86), channel_id=1, source_target_pairs={{0,1},{1,2},{2,3},{3,4},{4,5},{5,6},{6,7},{7,8},{8,9},{9,10},{10,1... | collective-permute-start | bytes 1191944 | tf_op jit(solution)/shard_map/ppermute | solution.py:462
  12.3 44.3 %copy-start.3 = (f32[12,8,8,128]{3,2,1,0:T(8,128)S(1)}, f32[12,8,8,128]{3,2,1,0:T(8,128)}, u32[]{:S(2)}) copy-start(f32[12,8,8,128]{3,2,1,0:T(8,128)} %param.12) | copy-start | bytes 1179652
  45.1 11.5 %copy-start.1 = (f32[12,8,8,128]{3,2,1,0:T(8,128)S(1)}, f32[12,8,8,128]{3,2,1,0:T(8,128)}, u32[]{:S(2)}) copy-start(f32[12,8,8,128]{3,2,1,0:T(8,128)} %param.11) | copy-start | bytes 1179652

commit v2 on v1

--- a/solution.py
+++ b/solution.py
@@ -117,6 +117,7 @@
         groups = -(-tiles // self.per_group)
         step = max(1, SUB // self.piece)
         self.groups = -(-groups // step) * step
+        self.whole_groups = self.coef_tiles // self.per_group
         self.chunk = self.groups * self.piece
         self.width = rows // self.piece
 
@@ -180,7 +181,7 @@
     return jnp.where(pos == 0, first, jnp.where(pos == q - 1, last, 0.0))
 
 
-def near_levels(plan, v, lo_ref, up_ref, prev_ref, next_ref):
+def near_levels(plan, v, coef):
     r = plan.rows
     at = lane()
     for k in plan.near:
@@ -193,15 +194,8 @@
         for t in (0, 1, 2) if k < plan.sent else (1,):
             low_sum = high_sum = None
             for b in range(SUB):
-                if t == 1:
-                    lc = lo_ref[pl.ds(64 * k + b, SUB, stride=SUB), :]
-                    uc = up_ref[pl.ds(64 * k + b, SUB, stride=SUB), :]
-                else:
-                    ref = prev_ref if t == 0 else next_ref
-                    lc = ref[pl.ds(64 * k + b, SUB, stride=SUB), :]
-                    uc = ref[pl.ds(64 * (plan.sent + k) + b, SUB, stride=SUB), :]
-                low = lc * spread(lower[t], b)
-                high = uc * spread(upper[t], b)
+                low = coef(t, 0, k, b) * spread(lower[t], b)
+                high = coef(t, 1, k, b) * spread(upper[t], b)
                 low_sum = low if low_sum is None else low_sum + low
                 high_sum = high if high_sum is None else high_sum + high
             fresh[t] = v[t] + low_sum + high_sum
@@ -213,26 +207,38 @@
     return jnp.where(sub() == 0, jnp.broadcast_to(total(u * u), u.shape), 0.0)
 
 
-def pack_kernel(plan, lo_ref, up_ref, rhs_ref, out_ref):
+def edge_kernel(plan, lo_ref, up_ref, rhs_ref, out_ref, sems):
     n = 64 * plan.sent
-    out_ref[pl.ds(0, n), :] = lo_ref[pl.ds(0, n), :]
-    out_ref[pl.ds(n, n), :] = up_ref[pl.ds(0, n), :]
-    out_ref[pl.ds(2 * n, SUB), :] = rhs_ref[...]
-
-
-def first_kernel(
-    plan, lo_ref, up_ref, fin_ref, dia_ref, bel_ref, abo_ref, rhs_ref, prev_ref, next_ref, out_ref, z_ref
-):
-    n = 64 * 2 * plan.sent
-    rhs = rhs_ref[...]
-    y = near_levels(
-        plan,
-        [prev_ref[pl.ds(n, SUB), :], rhs, next_ref[pl.ds(n, SUB), :]],
-        lo_ref,
-        up_ref,
-        prev_ref,
-        next_ref,
-    )
+    copies = [
+        pltpu.make_async_copy(lo_ref.at[pl.ds(0, n)], out_ref.at[pl.ds(0, n)], sems.at[0]),
+        pltpu.make_async_copy(up_ref.at[pl.ds(0, n)], out_ref.at[pl.ds(n, n)], sems.at[1]),
+        pltpu.make_async_copy(rhs_ref, out_ref.at[pl.ds(2 * n, SUB)], sems.at[2]),
+    ]
+    for c in copies:
+        c.start()
+    for c in copies:
+        c.wait()
+
+
+def pack_tile(plan, raw, index):
+    if index < plan.own_tiles:
+        return raw(index)
+    j = 2 * (index - plan.own_tiles)
+    a, b = halo_of(plan, raw(j)), halo_of(plan, raw(j + 1))
+    pos = lane() % plan.piece
+    moved = jnp.where(pos == 1, pltpu.roll(b, 1, 1), pltpu.roll(b, plan.rows - 1, 1))
+    return jnp.where((pos == 0) | (pos == plan.piece - 1), a, moved)
+
+
+def pack_group(plan, g, tiles, z_ref, out_ref):
+    z_ref[g % z_ref.shape[0]] = jnp.concatenate(tiles, 0).T
+    for i in range(plan.piece):
+        out_ref[pl.ds(g * plan.piece + i, plan.devices, stride=plan.chunk), :] = z_ref[
+            g % z_ref.shape[0], pl.ds(i, plan.devices, stride=plan.piece), :
+        ]
+
+
+def pack_kernel(plan, lo_ref, up_ref, fin_ref, dia_ref, bel_ref, abo_ref, out_ref, rest_ref, z_ref):
     mats = [(lo_ref, 64 * k) for k in plan.far] + [(up_ref, 64 * k) for k in plan.far]
     mats += [(fin_ref, 0), (dia_ref, 0), (bel_ref, 0), (abo_ref, 0)]
 
@@ -240,34 +246,45 @@
         ref, base = mats[index // SUB]
         return ref[pl.ds(base + index % SUB, SUB, stride=SUB), :]
 
-    def tile(index):
-        if index < plan.own_tiles:
-            return raw(index)
-        if index < plan.coef_tiles:
-            j = 2 * (index - plan.own_tiles)
-            a, b = halo_of(plan, raw(j)), halo_of(plan, raw(j + 1))
-            pos = lane() % plan.piece
-            moved = jnp.where(pos == 1, pltpu.roll(b, 1, 1), pltpu.roll(b, plan.rows - 1, 1))
-            return jnp.where((pos == 0) | (pos == plan.piece - 1), a, moved)
-        extra = index - plan.coef_tiles
-        if extra == 0:
-            return y
-        if extra == 1:
-            return halo_of(plan, y)
-        if extra == 2:
-            return square_tile(rhs)
-        if extra == 3:
-            return rhs
-        return jnp.zeros((SUB, plan.rows), jnp.float32)
-
-    g_tiles = plan.per_group
-    for g in range(plan.groups):
-        block = jnp.concatenate([tile(g * g_tiles + t) for t in range(g_tiles)], 0)
-        z_ref[g] = block.T
-        for i in range(plan.piece):
-            out_ref[pl.ds(g * plan.piece + i, plan.devices, stride=plan.chunk), :] = z_ref[
-                g, pl.ds(i, plan.devices, stride=plan.piece), :
-            ]
+    t = plan.per_group
+    for g in range(plan.whole_groups):
+        pack_group(plan, g, [pack_tile(plan, raw, g * t + i) for i in range(t)], z_ref, out_ref)
+    for i in range(plan.whole_groups * t, plan.coef_tiles):
+        rest_ref[i - plan.whole_groups * t] = pack_tile(plan, raw, i)
+
+
+def first_kernel(
+    plan, lo_ref, up_ref, rhs_ref, pair_ref, other_ref, rest_in_ref, chunk_ref, out_ref, coef_ref, field_ref, z_ref
+):
+    n = 64 * 2 * plan.sent
+    odd = lax.rem(lax.axis_index(AXIS), 2) == 1
+    rhs = rhs_ref[...]
+
+    def halo(t, start, stride):
+        a, b = pair_ref[pl.ds(start, SUB, stride=stride), :], other_ref[pl.ds(start, SUB, stride=stride), :]
+        return jnp.where(odd, a, b) if t == 0 else jnp.where(odd, b, a)
+
+    def coef(t, side, k, b):
+        if t == 1:
+            ref = up_ref if side else lo_ref
+            x = ref[pl.ds(64 * k + b, SUB, stride=SUB), :]
+        else:
+            x = halo(t, 64 * (plan.sent * side + k) + b, SUB)
+        coef_ref[t, side, k, b] = x
+        return x
+
+    fields = [halo(0, n, 1), rhs, halo(2, n, 1)]
+    for t in range(3):
+        field_ref[t] = fields[t]
+    y = near_levels(plan, fields, coef)
+    t = plan.per_group
+    first = plan.whole_groups * t
+    tiles = [rest_in_ref[i] for i in range(plan.coef_tiles - first)]
+    tiles += [y, halo_of(plan, y), square_tile(rhs), rhs]
+    tiles += [jnp.zeros_like(rhs)] * (plan.groups * t - first - len(tiles))
+    for g in range(plan.whole_groups, plan.groups):
+        at = g * t - first
+        pack_group(plan, g, tiles[at : at + t], z_ref, out_ref)
 
 
 def far_stage(plan, own, halo, coef_ref):
@@ -314,6 +331,74 @@
         dots = jnp.where(sub() == i, jnp.broadcast_to(total(v * w), w.shape), dots)
     send(plan, [before, w, after, dots], z_ref, out_ref)
     return w
+
+
+def two_sum(a, b):
+    s = a + b
+    t = s - a
+    return s, (a - (s - t)) + (b - t)
+
+
+def halves(a):
+    c = 4097.0 * a
+    hi = c - (c - a)
+    return hi, a - hi
+
+
+def two_prod(a, b):
+    p = a * b
+    ah, al = halves(a)
+    bh, bl = halves(b)
+    return p, ((ah * bh - p) + ah * bl + al * bh) + al * bl
+
+
+def pair_add(x, y):
+    s, e = two_sum(x[0], y[0])
+    e = e + (x[1] + y[1])
+    hi = s + e
+    return hi, e - (hi - s)
+
+
+def pair_mul(x, y):
+    p, e = two_prod(x[0], y[0])
+    e = e + (x[0] * y[1] + x[1] * y[0])
+    hi = p + e
+    return hi, e - (hi - p)
+
+
+def folded(x, shifts, axis):
+    for s in shifts:
+        x = pair_add(x, tuple(pltpu.roll(a, s, axis) for a in x))
+    return x
+
+
+def products():
+    out = [(i, None) for i in range(ITERS)] + [(None, None)]
+    return out + [(i, j) for i in range(ITERS) for j in range(i, ITERS)]
+
+
+def last_far_kernel(plan, in_ref, coef_ref, h_ref, w_in_ref, *rest):
+    j = ITERS - 1
+    vs = [v[...] for v in rest[:j]]
+    out_ref, s_ref, zr_ref, zs_ref = rest[j:]
+    y, halo, s, v = enter_far(plan, in_ref, h_ref, w_in_ref, vs, zr_ref)
+    s_ref[...] = s
+    vs = vs + [v]
+    w = far_stage(plan, y / s, halo / s, coef_ref)
+    sums = []
+    for a, b in products():
+        pair = two_prod(w if a is None else vs[a], w if b is None else vs[b])
+        sums.append(folded(pair, (4, 2, 1), 0))
+    at = sub()
+    packed = []
+    for start in range(0, len(sums), SUB):
+        tile = [jnp.zeros_like(w), jnp.zeros_like(w)]
+        for i, pair in enumerate(sums[start : start + SUB]):
+            tile = [jnp.where(at == i, x, old) for x, old in zip(pair, tile)]
+        packed.append(folded(tile, [2**i for i in range(plan.rows.bit_length() - 1)], 1))
+    (hi, lo), (hi2, lo2) = packed
+    last = jnp.where(at < SUB // 2, hi2, pltpu.roll(lo2, SUB // 2, 0))
+    send(plan, [w, hi, lo, last], zs_ref, out_ref)
 
 
 def start_far_kernel(plan, in_ref, out_ref, coef_ref, w_ref, v_ref, s_ref, z_ref, zs_ref):
@@ -357,18 +442,15 @@
     w_ref[...] = finish_far(plan, y, halo, s, [v], coef_ref, zs_ref, out_ref)
 
 
-def near_kernel(plan, j, in_ref, lo_ref, up_ref, rhs_ref, prev_ref, next_ref, *rest):
+def near_kernel(plan, j, in_ref, coef_ref, field_ref, *rest):
     us, ss = rest[: j - 1], rest[j - 1 : 2 * j - 1]
     out_ref, u_ref, h_ref, zr_ref, zs_ref = rest[2 * j - 1 :]
-    n = 64 * 2 * plan.sent
-    prev, own, nxt, dots = receive(plan, in_ref, zr_ref)
+    *w, dots = receive(plan, in_ref, zr_ref)
     pos = lane() % plan.piece
     h = jnp.sum(jnp.where(pos == 0, dots, 0.0), axis=1, keepdims=True) / plan.count
     h = jnp.broadcast_to(h, dots.shape)
     h_ref[...] = h
-    w = [prev, own, nxt]
-    fields = [[prev_ref[pl.ds(n, SUB), :], rhs_ref[...], next_ref[pl.ds(n, SUB), :]]]
-    fields += [[u[t] for t in range(3)] for u in us]
+    fields = [field_ref, *us]
     for t in range(3):
         acc = None
         for i in range(j):
@@ -376,55 +458,68 @@
             acc = term if acc is None else acc + term
         w[t] = w[t] - acc
         u_ref[t] = w[t]
-    y = near_levels(plan, w, lo_ref, up_ref, prev_ref, next_ref)
+    y = near_levels(plan, w, lambda t, side, k, b: coef_ref[t, side, k, b])
     send(plan, [y, halo_of(plan, y), square_tile(w[1])], zs_ref, out_ref)
+
+
+def enter_far(plan, in_ref, h_ref, w_in_ref, vs, z_ref):
+    y, halo, squares, _ = receive(plan, in_ref, z_ref)
+    s = norm_of(plan, squares)
+    h = h_ref[...]
+    acc = None
+    for i, v in enumerate(vs):
+        term = spread(h, i) * v
+        acc = term if acc is None else acc + term
+    return y, halo, s, (w_in_ref[...] - acc) / s
 
 
 def far_kernel(plan, j, in_ref, coef_ref, h_ref, w_in_ref, *rest):
     vs = [v[...] for v in rest[:j]]
     out_ref, w_ref, v_ref, s_ref, zr_ref, zs_ref = rest[j:]
-    y, halo, squares, _ = receive(plan, in_ref, zr_ref)
-    s = norm_of(plan, squares)
-    h = h_ref[...]
-    acc = None
-    for i in range(j):
-        term = spread(h, i) * vs[i]
-        acc = term if acc is None else acc + term
-    v = (w_in_ref[...] - acc) / s
+    y, halo, s, v = enter_far(plan, in_ref, h_ref, w_in_ref, vs, zr_ref)
     v_ref[...] = v
     s_ref[...] = s
     w_ref[...] = finish_far(plan, y, halo, s, vs + [v], coef_ref, zs_ref, out_ref)
 
 
-def last_kernel(plan, in_ref, rhs_ref, *rest):
-    us, ss = rest[: ITERS - 1], rest[ITERS - 1 : 2 * ITERS - 1]
-    u_ref, h_ref, out_ref, zr_ref = rest[2 * ITERS - 1 :]
-    _, own, _, dots = receive(plan, in_ref, zr_ref)
-    pos = lane() % plan.piece
-    h = jnp.sum(jnp.where(pos == 0, dots, 0.0), axis=1, keepdims=True) / plan.count
-    h = jnp.broadcast_to(h, dots.shape)
-    h_ref[...] = h
-    fields = [rhs_ref[...]] + [u[1] for u in us]
+def output_kernel(plan, in_ref, field_ref, *rest):
+    us = rest[: ITERS - 1]
+    ss = [s[...] for s in rest[ITERS - 1 : 2 * ITERS - 1]]
+    hs = [h[...] for h in rest[2 * ITERS - 1 : 3 * ITERS - 2]]
+    basis_ref, hess_ref, z_ref = rest[3 * ITERS - 2 :]
+    w, hi, lo, last = receive(plan, in_ref, z_ref)
+    shifts = [plan.piece * 2**i for i in range(plan.devices.bit_length() - 1)]
+    one = folded((hi, lo), shifts, 1)
+    two = folded((last, pltpu.roll(last, SUB // 2, 0)), shifts, 1)
+    sums = [tuple(x[i : i + 1] for x in one) for i in range(SUB)]
+    sums += [tuple(x[i : i + 1] for x in two) for i in range(SUB // 2)]
+    names = products()
+    got = dict(zip(names, sums))
+    h = [got[i, None][0] / plan.count for i in range(ITERS)]
+    zero = jnp.zeros_like(h[0])
+    squares = got[None, None]
+    for i in range(ITERS):
+        left = tuple(2.0 * x for x in got[i, None])
+        for j in range(ITERS):
+            left = pair_add(left, pair_mul((-h[j], zero), got[min(i, j), max(i, j)]))
+        squares = pair_add(squares, pair_mul((-h[i], zero), left))
+    squares = jnp.maximum(squares[0], 0.0)
+    wide = lambda x: jnp.broadcast_to(x, (SUB, plan.rows))
+    ss.append(wide(jnp.sqrt(squares / plan.count + EPS)))
+    fields = [field_ref[1]] + [u[1] for u in us]
+    vs = [f / s for f, s in zip(fields, ss)]
     acc = None
     for i in range(ITERS):
-        term = spread(h, i) * (fields[i] / ss[i][...])
+        term = wide(h[i]) * vs[i]
         acc = term if acc is None else acc + term
-    u = own - acc
-    u_ref[...] = u
-    out_ref[...] = jnp.broadcast_to(total(u * u), out_ref.shape)
-
-
-def output_kernel(plan, in_ref, rhs_ref, *rest):
-    us = [u[1] for u in rest[: ITERS - 1]] + [rest[ITERS - 1][...]]
-    ss = [s[...] for s in rest[ITERS : 2 * ITERS]]
-    hs = [h[...] for h in rest[2 * ITERS : 3 * ITERS]]
-    basis_ref, hess_ref = rest[3 * ITERS :]
-    squares = jnp.sum(in_ref[...], axis=0, keepdims=True)
-    ss.append(jnp.broadcast_to(jnp.sqrt(squares / plan.count + EPS), ss[0].shape))
-    fields = [rhs_ref[...]] + us
+    vs.append((w - acc) / ss[-1])
     for j in range(ITERS + 1):
-        basis_ref[j] = fields[j] / ss[j]
-    hess = jnp.zeros_like(ss[0])
+        basis_ref[j] = vs[j]
+    top = jnp.zeros_like(w)
+    for i in range(ITERS):
+        top = jnp.where(sub() == i, wide(h[i]), top)
+    hs.append(top)
+    hess = jnp.zeros_like(w)
     for j in range(ITERS):
         col = jnp.where(sub() <= j, hs[j], jnp.where(sub() == j + 1, ss[j + 1], 0.0))
         hess = jnp.where(lane() == j, col, hess)
@@ -442,15 +537,16 @@
     tile = shape(SUB, r)
     scratch = lambda *s: pltpu.VMEM(s, jnp.float32)
 
-    def call(kernel, outs, scratches, *args):
+    def call(kernel, outs, scratches, *args, space=pltpu.VMEM, flops=1_000_000, **more):
         return pl.pallas_call(
             kernel,
             out_shape=outs,
-            in_specs=[pl.BlockSpec(memory_space=pltpu.VMEM)] * len(args),
+            in_specs=[pl.BlockSpec(memory_space=space)] * len(args),
             out_specs=jax.tree.map(lambda _: pl.BlockSpec(memory_space=pltpu.VMEM), outs),
             scratch_shapes=scratches,
             compiler_params=pltpu.CompilerParams(vmem_limit_bytes=24 * 2**20),
-            cost_estimate=pl.CostEstimate(flops=4_000_000, bytes_accessed=2_000_000, transcendentals=0),
+            cost_estimate=pl.CostEstimate(flops=flops, bytes_accessed=1_000_000, transcendentals=0),
+            **more,
         )(*args)
 
     def exchange(x):
@@ -458,50 +554,61 @@
         return y.reshape(-1, r)
 
     part = functools.partial
-    edge = call(part(pack_kernel, plan), shape(64 * 2 * plan.sent + SUB, r), [], lo, up, right_side)
-    prev = lax.ppermute(edge, AXIS, [(i, i + 1) for i in range(d - 1)])
-    nxt = lax.ppermute(edge, AXIS, [(i + 1, i) for i in range(d - 1)])
-    big = call(
+    edge = call(
+        part(edge_kernel, plan),
+        shape(64 * 2 * plan.sent + SUB, r),
+        [pltpu.SemaphoreType.DMA((3,))],
+        lo, up, right_side,
+        space=pl.ANY,
+    )
+    other = lax.ppermute(edge, AXIS, [(i, i + 1 if i % 2 else i - 1) for i in range(1, d - 1)])
+    pair = lax.ppermute(edge, AXIS, [(i, i ^ 1) for i in range(d)])
+    left = plan.coef_tiles - plan.whole_groups * plan.per_group
+    chunk, rest = call(
+        part(pack_kernel, plan),
+        (shape(d * plan.chunk, r), shape(max(left, 1), SUB, r)),
+        [scratch(plan.whole_groups, r, r)],
+        lo, up, fin, dia, bel, abo,
+        flops=20_000_000,
+    )
+    chunk, near, fields = call(
         part(first_kernel, plan),
-        shape(d * plan.chunk, r),
-        [scratch(plan.groups, r, r)],
-        lo, up, fin, dia, bel, abo, right_side, prev, nxt,
+        (shape(d * plan.chunk, r), shape(3, 2, len(plan.near), SUB, SUB, r), shape(3, SUB, r)),
+        [scratch(plan.groups - plan.whole_groups, r, r)],
+        lo, up, right_side, pair, other, rest, chunk,
+        input_output_aliases={6: 0},
     )
-    got = exchange(big)
     small = shape(d, r)
+    two = [scratch(r, r), scratch(r, r)]
     out, coef, w, v, s = call(
         part(start_far_kernel, plan),
         (small, shape(plan.own_tiles + plan.halo_tiles, SUB, r), tile, tile, tile),
         [scratch(plan.groups, r, r), scratch(r, r)],
-        got,
+        exchange(chunk),
     )
     us, ss, vs, hs = [], [s], [v], []
     for j in range(1, ITERS):
         out, u, h = call(
             part(near_kernel, plan, j),
             (small, shape(3, SUB, r), tile),
-            [scratch(r, r), scratch(r, r)],
-            exchange(out), lo, up, right_side, prev, nxt, *us, *ss,
+            two,
+            exchange(out), near, fields, *us, *ss,
         )
         us.append(u)
         hs.append(h)
-        out, w, v, s = call(
-            part(far_kernel, plan, j),
-            (small, tile, tile, tile),
-            [scratch(r, r), scratch(r, r)],
-            exchange(out), coef, h, w, *vs,
-        )
-        vs.append(v)
+        if j < ITERS - 1:
+            out, w, v, s = call(
+                part(far_kernel, plan, j), (small, tile, tile, tile), two, exchange(out), coef, h, w, *vs
+            )
+            vs.append(v)
+        else:
+            out, s = call(part(last_far_kernel, plan), (small, tile), two, exchange(out), coef, h, w, *vs)
         ss.append(s)
-    u, h, out = call(
-        part(last_kernel, plan), (tile, tile, small), [scratch(r, r)], exchange(out), right_side, *us, *ss
-    )
-    hs.append(h)
     return call(
         part(output_kernel, plan),
         (shape(ITERS + 1, SUB, r), shape(ITERS + 1, ITERS)),
-        [],
-        exchange(out), right_side, *us, u, *ss, *hs,
+        [scratch(r, r)],
+        exchange(out), fields, *us, *ss, *hs,
     )
 
 

time: 107 us -> 96.6 us (0.903)
  blocking collectives: 87.6 us -> 73.6 us
  local copies, waits for them, and re-layouts: 2.7 us -> 5.7 us
  waiting for transfers between devices: 1.3 us -> 0.01 us
  Pallas kernels: 9.69 us -> 10.9 us
    all_to_all x7 -> x6, blocking collectives: 87.6 us -> 73.6 us  [exchange(): y = lax.all_to_all(x.reshape(d, -1, r), AXIS, 0, 0)]
    unnamed x18 -> x16, local copies, waits for them, and re-layouts: 2.7 us -> 5.7 us
    ppermute x2, waiting for transfers between devices: 1.3 us -> 0.01 us  [the longest x1 0.01 us: transposed(): lax.ppermute(edge, AXIS, [(i, i + 1 if i % 2 else i - 1) for i in range(1...]
    pallas_call x9, Pallas kernels: 9.69 us -> 10.9 us  [call(): pl.pallas_call(kernel, out_shape=outs, in_specs=[pl.BlockSpec(memory_spac...]
  transfers between devices with their start and end apart: 2 -> 2, of which waited for: 1 -> 0; matrix products, arithmetic and copies ran while one was open for 0% -> 0% of each run, Pallas kernels for 0% -> 3%
where the time goes in v2:
time: 96.6 us; the launch traced here: 96 us
  blocking collectives  73.6 us (76%)
  Pallas kernels  10.9 us (11%)
  local copies, waits for them, and re-layouts  5.7 us (6%)
  starting transfers between devices  5.06 us (5%)
    all_to_all x6, blocking collectives, exchange(): y = lax.all_to_all(x.reshape(d, -1, r), AXIS, 0, 0)  73.6 us
    pallas_call x9, Pallas kernels, call(): pl.pallas_call(kernel, out_shape=outs, in_specs=[pl.BlockSpec(memory_spac...  10.9 us
    unnamed x16, local copies, waits for them, and re-layouts  5.7 us
    ppermute x1, starting transfers between devices, transposed(): pair = lax.ppermute(edge, AXIS, [(i, i ^ 1) for i in range(d)])  4.37 us
  transfers between devices with their start and end apart: 2, of which 0 were waited for; matrix products, arithmetic and copies ran while one was open for 0% of the time, Pallas kernels for 3%

profile of v2, /device:TPU:0, one launch (start us, length us, event | category | flops | bytes accessed | tf_op | source)
XLA Modules:
  0.0 96.0 jit_solution(11065093830183154423)
XLA Ops:
  0.6 0.0 copy-start
  0.6 1.0 %copy-done = f32[12,8,8,128]{3,2,1,0:T(8,128)S(1)} copy-done((f32[12,8,8,128]{3,2,1,0:T(8,128)S(1)}, f32[12,8,8,128]{3,2,1,0:T(8,128)}, u32[]{:S(2)}) %copy-start) | copy-done | bytes 393240
  1.6 0.0 copy-start.1
  1.6 1.0 %copy-done.1 = f32[12,8,8,128]{3,2,1,0:T(8,128)S(1)} copy-done((f32[12,8,8,128]{3,2,1,0:T(8,128)S(1)}, f32[12,8,8,128]{3,2,1,0:T(8,128)}, u32[]{:S(2)}) %copy-start.1) | copy-done | bytes 393240
  2.6 0.0 copy-start.6
  2.6 0.7 copy-done.6
  3.3 0.0 copy-start.7
  3.3 0.5 shard_map.86
  3.8 0.7 collective-permute-start.1
  4.5 4.4 %collective-permute-start = (f32[776,128]{1,0:T(8,128)S(1)}, f32[776,128]{1,0:T(8,128)S(1)}, u32[]{:S(2)}, u32[]{:S(2)}) collective-permute-start(f32[776,128]{1,0:T(8,128)S(1)} %shard_map.86), channel_id=1, source_target_pairs={{0,1},{1,0},{2,3},{3,2},{4,5},{5,4},{6,7},{7,6},{8,9},{9,8},{10,11... | collective-permute-start | bytes 1191944 | tf_op jit(solution)/shard_map/ppermute | solution.py:565
  8.9 0.0 copy-start.2
  8.9 0.8 copy-done.2
  9.7 0.0 copy-start.3
  9.7 0.8 copy-done.3
  10.4 0.0 copy-start.4
  10.4 0.8 copy-done.4
  11.2 0.0 copy-start.5
  11.2 0.8 copy-done.5
  11.9 2.7 %shard_map.87 = (f32[1280,128]{1,0:T(8,128)S(1)}, f32[12,8,128]{2,1,0:T(8,128)S(1)}) custom-call(f32[768,128]{1,0:T(8,128)S(1)} %bitcast.29, f32[768,128]{1,0:T(8,128)S(1)} %bitcast.32, f32[64,128]{1,0:T(8,128)S(1)} %bitcast.41, f32[64,128]{1,0:T(8,128)S(1)} %bitcast.42, f32[64,128]{1,0:T(8,128)S(1)} %bitcast.43, f32[64,128]{1,0:T(8,128)S(1)} %bitcast.44), custom_call_target="tpu_custom_call" | custom-call | flops 20000000 | bytes 1000000 | tf_op jit(solution)/shard_map/pallas_call | solution.py:541
  14.6 0.0 collective-permute-done.1.other_ref
  14.6 0.0 collective-permute-done.pair_ref
  14.6 0.0 copy-done.7
  14.6 0.8 shard_map.88
  15.4 27.7 %all_to_all.30 = f32[32,40,128]{2,1,0:T(8,128)S(1)} all-to-all(f32[32,40,128]{2,1,0:T(8,128)S(1)} %bitcast.35), channel_id=1, replica_groups=mesh['chain'=32] {'chain'}, dimensions={0} | all-to-all | bytes 1310720 | tf_op jit(solution)/shard_map/all_to_all | solution.py:553
  43.1 1.1 %shard_map.89 = (f32[32,128]{1,0:T(8,128)S(1)}, f32[200,8,128]{2,1,0:T(8,128)S(1)}, f32[8,128]{1,0:T(8,128)S(1)}, f32[8,128]{1,0:T(8,128)S(1)}, f32[8,128]{1,0:T(8,128)S(1)}) custom-call(f32[1280,128]{1,0:T(8,128)S(1)} %bitcast.34), custom_call_target="tpu_custom_call" | custom-call | flops 1000000 | bytes 1000000 | tf_op jit(solution)/shard_map/pallas_call | solution.py:541
  44.2 10.4 %all_to_all.31 = f32[32,1,128]{2,1,0:T(1,128)S(1)} all-to-all(f32[32,1,128]{2,1,0:T(1,128)S(1)} %bitcast.46), channel_id=1, replica_groups=mesh['chain'=32] {'chain'}, dimensions={0} | all-to-all | bytes 32768 | tf_op jit(solution)/shard_map/all_to_all | solution.py:553
  54.6 1.1 %shard_map.90 = (f32[32,128]{1,0:T(8,128)S(1)}, f32[3,8,128]{2,1,0:T(8,128)S(1)}, f32[8,128]{1,0:T(8,128)S(1)}) custom-call(f32[32,128]{1,0:T(8,128)S(1)} %bitcast.37, f32[3,2,7,8,8,128]{5,4,3,2,1,0:T(8,128)S(1)} %get-tuple-element.28.coef_ref, f32[3,8,128]{2,1,0:T(8,128)S(1)} %get-tuple-element.29.field_ref, ...), custom_call_target="tpu_custom_call" | custom-call | flops 1000000 | bytes 1000000 | tf_op jit(solution)/shard_map/pallas_call | solution.py:541
  55.7 8.9 %all_to_all.32 = f32[32,1,128]{2,1,0:T(1,128)S(1)} all-to-all(f32[32,1,128]{2,1,0:T(1,128)S(1)} %bitcast.49), channel_id=1, replica_groups=mesh['chain'=32] {'chain'}, dimensions={0} | all-to-all | bytes 32768 | tf_op jit(solution)/shard_map/all_to_all | solution.py:553
  64.5 1.0 %shard_map.91 = (f32[32,128]{1,0:T(8,128)S(1)}, f32[8,128]{1,0:T(8,128)S(1)}, f32[8,128]{1,0:T(8,128)S(1)}, f32[8,128]{1,0:T(8,128)S(1)}) custom-call(f32[32,128]{1,0:T(8,128)S(1)} %bitcast.38, f32[200,8,128]{2,1,0:T(8,128)S(1)} %get-tuple-element.32.coef_ref, f32[8,128]{1,0:T(8,128)S(1)} %get-tuple-element.33.h_ref.rest_5_, ...), custom_call_target="tpu_custom_call" | custom-call | flops 1000000 | bytes 1000000 | tf_op jit(solution)/shard_map/pallas_call | solution.py:541
  65.6 8.9 %all_to_all.33 = f32[32,1,128]{2,1,0:T(1,128)S(1)} all-to-all(f32[32,1,128]{2,1,0:T(1,128)S(1)} %bitcast.47), channel_id=1, replica_groups=mesh['chain'=32] {'chain'}, dimensions={0} | all-to-all | bytes 32768 | tf_op jit(solution)/shard_map/all_to_all | solution.py:553
  74.4 1.1 %shard_map.92 = (f32[32,128]{1,0:T(8,128)S(1)}, f32[3,8,128]{2,1,0:T(8,128)S(1)}, f32[8,128]{1,0:T(8,128)S(1)}) custom-call(f32[32,128]{1,0:T(8,128)S(1)} %bitcast.36, f32[3,2,7,8,8,128]{5,4,3,2,1,0:T(8,128)S(1)} %get-tuple-element.28.coef_ref, f32[3,8,128]{2,1,0:T(8,128)S(1)} %get-tuple-element.29.field_ref, f32[3,8,128]{2,1,0:T(8,128)S(1)} %get-tuple-element.37.rest_0_, ...), custom_call_target="tpu_custom_call" | custom-call | flops 1000000 | bytes 1000000 | tf_op jit(solution)/shard_map/pallas_call | solution.py:541
  75.5 8.9 %all_to_all.34 = f32[32,1,128]{2,1,0:T(1,128)S(1)} all-to-all(f32[32,1,128]{2,1,0:T(1,128)S(1)} %bitcast.48), channel_id=1, replica_groups=mesh['chain'=32] {'chain'}, dimensions={0} | all-to-all | bytes 32768 | tf_op jit(solution)/shard_map/all_to_all | solution.py:553
  84.4 1.5 %shard_map.93 = (f32[32,128]{1,0:T(8,128)S(1)}, f32[8,128]{1,0:T(8,128)S(1)}) custom-call(f32[32,128]{1,0:T(8,128)S(1)} %bitcast.40, f32[200,8,128]{2,1,0:T(8,128)S(1)} %get-tuple-element.32.coef_ref, f32[8,128]{1,0:T(8,128)S(1)} %get-tuple-element.40.h_ref.rest_6_, f32[8,128]{1,0:T(8,128)S(1)} %get-tuple-element.41.w_in_ref, ...), custom_call_target="tpu_custom_call" | custom-call | flops 1000000 | bytes 1000000 | tf_op jit(solution)/shard_map/pallas_call | solution.py:541
  85.9 8.9 %all_to_all.35 = f32[32,1,128]{2,1,0:T(1,128)S(1)} all-to-all(f32[32,1,128]{2,1,0:T(1,128)S(1)} %bitcast.45), channel_id=1, replica_groups=mesh['chain'=32] {'chain'}, dimensions={0} | all-to-all | bytes 32768 | tf_op jit(solution)/shard_map/all_to_all | solution.py:553
  94.7 1.2 %shard_map.94 = (f32[4,8,128]{2,1,0:T(8,128)}, f32[4,3]{1,0:T(4,128)}) custom-call(f32[32,128]{1,0:T(8,128)S(1)} %bitcast.39, f32[3,8,128]{2,1,0:T(8,128)S(1)} %get-tuple-element.29.field_ref, f32[3,8,128]{2,1,0:T(8,128)S(1)} %get-tuple-element.37.rest_0_, f32[3,8,128]{2,1,0:T(8,128)S(1)} %get-tuple-element.44.rest_1_, ...), custom_call_target="tpu_custom_call" | custom-call | flops 1000000 | bytes 1000000 | tf_op jit(solution)/shard_map/pallas_call | solution.py:541
Async XLA Ops:
  0.6 1.0 %copy-start = (f32[12,8,8,128]{3,2,1,0:T(8,128)S(1)}, f32[12,8,8,128]{3,2,1,0:T(8,128)}, u32[]{:S(2)}) copy-start(f32[12,8,8,128]{3,2,1,0:T(8,128)} %param.11) | copy-start | bytes 1179652
  1.6 1.0 %copy-start.1 = (f32[12,8,8,128]{3,2,1,0:T(8,128)S(1)}, f32[12,8,8,128]{3,2,1,0:T(8,128)}, u32[]{:S(2)}) copy-start(f32[12,8,8,128]{3,2,1,0:T(8,128)} %param.12) | copy-start | bytes 1179652
  2.6 0.7 copy-start.6
  3.3 11.3 %copy-start.7 = (f32[8,128]{1,0:T(8,128)S(1)}, f32[8,128]{1,0:T(8,128)}, u32[]{:S(2)}) copy-start(f32[8,128]{1,0:T(8,128)} %rhs_ref.3) | copy-start | bytes 12292
  3.8 10.8 %collective-permute-start.1 = (f32[776,128]{1,0:T(8,128)S(1)}, f32[776,128]{1,0:T(8,128)S(1)}, u32[]{:S(2)}, u32[]{:S(2)}) collective-permute-start(f32[776,128]{1,0:T(8,128)S(1)} %shard_map.86), channel_id=1, source_target_pairs={{1,2},{2,1},{3,4},{4,3},{5,6},{6,5},{7,8},{8,7},{9,10},{10,9},{11,... | collective-permute-start | bytes 1191944 | tf_op jit(solution)/shard_map/ppermute | solution.py:564
  4.5 10.1 %collective-permute-start = (f32[776,128]{1,0:T(8,128)S(1)}, f32[776,128]{1,0:T(8,128)S(1)}, u32[]{:S(2)}, u32[]{:S(2)}) collective-permute-start(f32[776,128]{1,0:T(8,128)S(1)} %shard_map.86), channel_id=1, source_target_pairs={{0,1},{1,0},{2,3},{3,2},{4,5},{5,4},{6,7},{7,6},{8,9},{9,8},{10,11... | collective-permute-start | bytes 1191944 | tf_op jit(solution)/shard_map/ppermute | solution.py:565
  8.9 0.8 copy-start.2
  9.7 0.8 copy-start.3
  10.4 0.8 copy-start.4
  11.2 0.8 copy-start.5

commit v3 on v2

--- a/solution.py
+++ b/solution.py
@@ -7,12 +7,14 @@
 from jax.experimental.pallas import tpu as pltpu
 from jax.sharding import PartitionSpec as P
 
+
 ITERS = 3
 
 
 EPS = 1e-06
 AXIS = "chain"
 SUB = 8
+EARLY = 6
 
 
 def padded_2(x, sides, width):
@@ -118,7 +120,7 @@
         step = max(1, SUB // self.piece)
         self.groups = -(-groups // step) * step
         self.whole_groups = self.coef_tiles // self.per_group
-        self.chunk = self.groups * self.piece
+        self.early = self.whole_groups * EARLY // 8 // step * step
         self.width = rows // self.piece
 
 
@@ -207,13 +209,18 @@
     return jnp.where(sub() == 0, jnp.broadcast_to(total(u * u), u.shape), 0.0)
 
 
-def edge_kernel(plan, lo_ref, up_ref, rhs_ref, out_ref, sems):
+def load_kernel(plan, *refs):
+    count = (len(refs) - 2) // 2
+    ins, outs, edge_ref, sems = refs[:count], refs[count:-2], refs[-2], refs[-1]
+    rhs_ref, lo_ref, up_ref = ins[:3]
     n = 64 * plan.sent
-    copies = [
-        pltpu.make_async_copy(lo_ref.at[pl.ds(0, n)], out_ref.at[pl.ds(0, n)], sems.at[0]),
-        pltpu.make_async_copy(up_ref.at[pl.ds(0, n)], out_ref.at[pl.ds(n, n)], sems.at[1]),
-        pltpu.make_async_copy(rhs_ref, out_ref.at[pl.ds(2 * n, SUB)], sems.at[2]),
+    pairs = [
+        (lo_ref.at[pl.ds(0, n)], edge_ref.at[pl.ds(0, n)]),
+        (up_ref.at[pl.ds(0, n)], edge_ref.at[pl.ds(n, n)]),
+        (rhs_ref, edge_ref.at[pl.ds(2 * n, SUB)]),
     ]
+    pairs += list(zip(ins, outs))
+    copies = [pltpu.make_async_copy(x, y, sems.at[i]) for i, (x, y) in enumerate(pairs)]
     for c in copies:
         c.start()
     for c in copies:
@@ -230,15 +237,16 @@
     return jnp.where((pos == 0) | (pos == plan.piece - 1), a, moved)
 
 
-def pack_group(plan, g, tiles, z_ref, out_ref):
-    z_ref[g % z_ref.shape[0]] = jnp.concatenate(tiles, 0).T
+def pack_group(plan, at, rows, tiles, z_ref, slot, out_ref):
+    z_ref[slot] = jnp.concatenate(tiles, 0).T
     for i in range(plan.piece):
-        out_ref[pl.ds(g * plan.piece + i, plan.devices, stride=plan.chunk), :] = z_ref[
-            g % z_ref.shape[0], pl.ds(i, plan.devices, stride=plan.piece), :
+        out_ref[pl.ds(at * plan.piece + i, plan.devices, stride=rows), :] = z_ref[
+            slot, pl.ds(i, plan.devices, stride=plan.piece), :
         ]
 
 
-def pack_kernel(plan, lo_ref, up_ref, fin_ref, dia_ref, bel_ref, abo_ref, out_ref, rest_ref, z_ref):
+def pack_kernel(plan, first, last, lo_ref, up_ref, fin_ref, dia_ref, bel_ref, abo_ref, out_ref, *rest):
+    z_ref = rest[-1]
     mats = [(lo_ref, 64 * k) for k in plan.far] + [(up_ref, 64 * k) for k in plan.far]
     mats += [(fin_ref, 0), (dia_ref, 0), (bel_ref, 0), (abo_ref, 0)]
 
@@ -247,10 +255,12 @@
         return ref[pl.ds(base + index % SUB, SUB, stride=SUB), :]
 
     t = plan.per_group
-    for g in range(plan.whole_groups):
-        pack_group(plan, g, [pack_tile(plan, raw, g * t + i) for i in range(t)], z_ref, out_ref)
-    for i in range(plan.whole_groups * t, plan.coef_tiles):
-        rest_ref[i - plan.whole_groups * t] = pack_tile(plan, raw, i)
+    rows = out_ref.shape[0] // plan.devices
+    for g in range(first, last):
+        pack_group(plan, g - first, rows, [pack_tile(plan, raw, g * t + i) for i in range(t)], z_ref, g - first, out_ref)
+    if len(rest) > 1:
+        for i in range(last * t, plan.coef_tiles):
+            rest[0][i - last * t] = pack_tile(plan, raw, i)
 
 
 def first_kernel(
@@ -282,9 +292,10 @@
     tiles = [rest_in_ref[i] for i in range(plan.coef_tiles - first)]
     tiles += [y, halo_of(plan, y), square_tile(rhs), rhs]
     tiles += [jnp.zeros_like(rhs)] * (plan.groups * t - first - len(tiles))
+    rows = out_ref.shape[0] // plan.devices
     for g in range(plan.whole_groups, plan.groups):
-        at = g * t - first
-        pack_group(plan, g, tiles[at : at + t], z_ref, out_ref)
+        at, slot = g * t - first, g - plan.whole_groups
+        pack_group(plan, g - plan.early, rows, tiles[at : at + t], z_ref, slot, out_ref)
 
 
 def far_stage(plan, own, halo, coef_ref):
@@ -401,7 +412,7 @@
     send(plan, [w, hi, lo, last], zs_ref, out_ref)
 
 
-def start_far_kernel(plan, in_ref, out_ref, coef_ref, w_ref, v_ref, s_ref, z_ref, zs_ref):
+def start_far_kernel(plan, early_ref, late_ref, out_ref, coef_ref, w_ref, v_ref, s_ref, z_ref, zs_ref):
     q, r = plan.piece, plan.rows
     at = lane()
     pos = at % q
@@ -409,9 +420,11 @@
     g_tiles = plan.per_group
     extra = []
     for g in range(plan.groups):
+        in_ref, at_group = (early_ref, g) if g < plan.early else (late_ref, g - plan.early)
+        rows = in_ref.shape[0] // plan.devices
         for i in range(q):
             z_ref[g, pl.ds(i, plan.devices, stride=q), :] = in_ref[
-                pl.ds(g * q + i, plan.devices, stride=plan.chunk), :
+                pl.ds(at_group * q + i, plan.devices, stride=rows), :
             ]
         t = z_ref[g].T
         for j in range(g_tiles):
@@ -554,28 +567,41 @@
         return y.reshape(-1, r)
 
     part = functools.partial
-    edge = call(
-        part(edge_kernel, plan),
-        shape(64 * 2 * plan.sent + SUB, r),
-        [pltpu.SemaphoreType.DMA((3,))],
-        lo, up, right_side,
-        space=pl.ANY,
+    raw = tuple(pltpu.with_memory_space_constraint(x, pltpu.HBM) for x in (right_side, lo, up, fin, dia, bel, abo))
+    *loaded, edge = call(
+        part(load_kernel, plan),
+        (*(shape(*x.shape) for x in raw), shape(64 * 2 * plan.sent + SUB, r)),
+        [pltpu.SemaphoreType.DMA((len(raw) + 3,))],
+        *raw,
+        space=pltpu.HBM,
     )
+    rhs, lo, up = loaded[:3]
+    mats = loaded[1:]
     other = lax.ppermute(edge, AXIS, [(i, i + 1 if i % 2 else i - 1) for i in range(1, d - 1)])
     pair = lax.ppermute(edge, AXIS, [(i, i ^ 1) for i in range(d)])
+    rows_of = lambda groups: d * groups * plan.piece
+    early = call(
+        part(pack_kernel, plan, 0, plan.early),
+        shape(rows_of(plan.early), r),
+        [scratch(plan.early, r, r)],
+        *mats,
+        flops=10_000_000,
+    )
+    early = exchange(early)
     left = plan.coef_tiles - plan.whole_groups * plan.per_group
-    chunk, rest = call(
-        part(pack_kernel, plan),
-        (shape(d * plan.chunk, r), shape(max(left, 1), SUB, r)),
-        [scratch(plan.whole_groups, r, r)],
-        lo, up, fin, dia, bel, abo,
-        flops=20_000_000,
+    late_shape = shape(rows_of(plan.groups - plan.early), r)
+    late, rest = call(
+        part(pack_kernel, plan, plan.early, plan.whole_groups),
+        (late_shape, shape(max(left, 1), SUB, r)),
+        [scratch(plan.whole_groups - plan.early, r, r)],
+        *mats,
+        flops=10_000_000,
     )
-    chunk, near, fields = call(
+    late, near, fields = call(
         part(first_kernel, plan),
-        (shape(d * plan.chunk, r), shape(3, 2, len(plan.near), SUB, SUB, r), shape(3, SUB, r)),
+        (late_shape, shape(3, 2, len(plan.near), SUB, SUB, r), shape(3, SUB, r)),
         [scratch(plan.groups - plan.whole_groups, r, r)],
-        lo, up, right_side, pair, other, rest, chunk,
+        lo, up, rhs, pair, other, rest, late,
         input_output_aliases={6: 0},
     )
     small = shape(d, r)
@@ -584,7 +610,7 @@
         part(start_far_kernel, plan),
         (small, shape(plan.own_tiles + plan.halo_tiles, SUB, r), tile, tile, tile),
         [scratch(plan.groups, r, r), scratch(r, r)],
-        exchange(chunk),
+        early, exchange(late),
     )
     us, ss, vs, hs = [], [s], [v], []
     for j in range(1, ITERS):

time: 96.6 us -> 94.2 us (0.975)
  blocking collectives: 73.6 us -> 63.3 us
  waiting for transfers between devices: 0.01 us -> 9.18 us
  local copies, waits for them, and re-layouts: 5.7 us -> 0 us
  starting transfers between devices: 5.06 us -> 8.32 us
  Pallas kernels: 10.9 us -> 12.4 us
    all_to_all x6, blocking collectives: 73.6 us -> 63.3 us  [exchange(): y = lax.all_to_all(x.reshape(d, -1, r), AXIS, 0, 0)]
    all_to_all x0 -> x1, waiting for transfers between devices: none -> 9.18 us  [exchange(): y = lax.all_to_all(x.reshape(d, -1, r), AXIS, 0, 0)]
    all_to_all x0 -> x1, starting transfers between devices: none -> 7.33 us  [exchange(): y = lax.all_to_all(x.reshape(d, -1, r), AXIS, 0, 0)]
    unnamed x16 -> x0, local copies, waits for them, and re-layouts: 5.7 us -> none
    ppermute x1, starting transfers between devices: 4.37 us -> 0.32 us  [transposed(): pair = lax.ppermute(edge, AXIS, [(i, i ^ 1) for i in range(d)])]
    pallas_call x9 -> x10, Pallas kernels: 10.9 us -> 12.4 us  [call(): pl.pallas_call(kernel, out_shape=outs, in_specs=[pl.BlockSpec(memory_spac...]
  transfers between devices with their start and end apart: 2 -> 3, of which waited for: 0 -> 1; matrix products, arithmetic and copies ran while one was open for 0% -> 0% of each run, Pallas kernels for 3% -> 3%
where the time goes in v3:
time: 94.2 us; the launch traced here: 93.9 us
  blocking collectives  63.3 us (67%)
  Pallas kernels  12.4 us (13%)
  waiting for transfers between devices  9.18 us (10%)
  starting transfers between devices  8.32 us (9%)
    all_to_all x6, blocking collectives, exchange(): y = lax.all_to_all(x.reshape(d, -1, r), AXIS, 0, 0)  63.3 us
    pallas_call x10, Pallas kernels, call(): pl.pallas_call(kernel, out_shape=outs, in_specs=[pl.BlockSpec(memory_spac...  12.4 us
    all_to_all x1, waiting for transfers between devices, exchange(): y = lax.all_to_all(x.reshape(d, -1, r), AXIS, 0, 0)  9.18 us
    all_to_all x1, starting transfers between devices, exchange(): y = lax.all_to_all(x.reshape(d, -1, r), AXIS, 0, 0)  7.33 us
  transfers between devices with their start and end apart: 3, of which 1 were waited for; matrix products, arithmetic and copies ran while one was open for 0% of the time, Pallas kernels for 3%

profile of v3, /device:TPU:0, one launch (start us, length us, event | category | flops | bytes accessed | tf_op | source)
XLA Modules:
  0.0 93.9 jit_solution(1341605197904923823)
XLA Ops:
  0.6 1.4 %shard_map.86 = (f32[8,128]{1,0:T(8,128)S(1)}, f32[768,128]{1,0:T(8,128)S(1)}, f32[768,128]{1,0:T(8,128)S(1)}, f32[64,128]{1,0:T(8,128)S(1)}, f32[64,128]{1,0:T(...) custom-call(f32[8,128]{1,0:T(8,128)} %refs_0_.1, f32[768,128]{1,0:T(8,128)} %bitcast.43, ...), custom_call_target="tpu_custom_call" | custom-call | flops 1000000 | bytes 1000000 | tf_op jit(solution)/shard_map/pallas_call | solution.py:554
  2.1 0.9 %shard_map.87 = f32[768,128]{1,0:T(8,128)} custom-call(f32[768,128]{1,0:T(8,128)S(1)} %get-tuple-element.32.lo_ref, f32[768,128]{1,0:T(8,128)S(1)} %get-tuple-element.33.up_ref, f32[64,128]{1,0:T(8,128)S(1)} %get-tuple-element.34.fin_ref, f32[64,128]{1,0:T(8,128)S(1)} %get-tuple-element.35.dia_ref, f32[64,128]{1,0:T(8,128)S(1)} %get-tuple-element.36.bel_ref, ...), custom_call_target="tpu_custom_call" | custom-call | flops 10000000 | bytes 1000000 | tf_op jit(solution)/shard_map/pallas_call | solution.py:554
  3.0 7.3 %all-to-all-start = ((f32[32,24,128]{2,1,0:T(8,128)}), f32[32,24,128]{2,1,0:T(8,128)S(1)}, u32[]{:S(2)}, u32[]{:S(2)}) async-start(f32[32,24,128]{2,1,0:T(8,128)} %bitcast.6), calls=%async_computation | async-start | bytes 786432 | tf_op jit(solution)/shard_map/all_to_all | solution.py:566
  10.4 0.3 collective-permute-start
  10.7 0.7 collective-permute-start.1
  11.4 2.3 %shard_map.88 = (f32[512,128]{1,0:T(8,128)S(1)}, f32[12,8,128]{2,1,0:T(8,128)S(1)}) custom-call(f32[768,128]{1,0:T(8,128)S(1)} %get-tuple-element.32.lo_ref, f32[768,128]{1,0:T(8,128)S(1)} %get-tuple-element.33.up_ref, f32[64,128]{1,0:T(8,128)S(1)} %get-tuple-element.34.fin_ref, f32[64,128]{1,0:T(8,128)S(1)} %get-tuple-element.35.dia_ref, ...), custom_call_target="tpu_custom_call" | custom-call | flops 10000000 | bytes 1000000 | tf_op jit(solution)/shard_map/pallas_call | solution.py:554
  13.6 0.0 collective-permute-done.pair_ref
  13.6 0.0 collective-permute-done.1.other_ref
  13.6 0.8 shard_map.89
  14.4 9.2 %all-to-all-done = f32[32,24,128]{2,1,0:T(8,128)S(1)} async-done(((f32[32,24,128]{2,1,0:T(8,128)}), f32[32,24,128]{2,1,0:T(8,128)S(1)}, u32[]{:S(2)}, u32[]{:S(2)}) %all-to-all-start) | async-done | bytes 393248 | tf_op jit(solution)/shard_map/all_to_all | solution.py:566
  23.6 18.4 %all_to_all.35 = f32[32,16,128]{2,1,0:T(8,128)S(1)} all-to-all(f32[32,16,128]{2,1,0:T(8,128)S(1)} %bitcast.32), channel_id=1, replica_groups=mesh['chain'=32] {'chain'}, dimensions={0} | all-to-all | bytes 524288 | tf_op jit(solution)/shard_map/all_to_all | solution.py:566
  42.0 1.1 %shard_map.90 = (f32[32,128]{1,0:T(8,128)S(1)}, f32[200,8,128]{2,1,0:T(8,128)S(1)}, f32[8,128]{1,0:T(8,128)S(1)}, f32[8,128]{1,0:T(8,128)S(1)}, f32[8,128]{1,0:T(8,128)S(1)}) custom-call(f32[768,128]{1,0:T(8,128)S(1)} %bitcast.30, f32[512,128]{1,0:T(8,128)S(1)} %bitcast.31), custom_call_target="tpu_custom_call" | custom-call | flops 1000000 | bytes 1000000 | tf_op jit(solution)/shard_map/pallas_call | solution.py:554
  43.2 9.4 %all_to_all.36 = f32[32,1,128]{2,1,0:T(1,128)S(1)} all-to-all(f32[32,1,128]{2,1,0:T(1,128)S(1)} %bitcast.38), channel_id=1, replica_groups=mesh['chain'=32] {'chain'}, dimensions={0} | all-to-all | bytes 32768 | tf_op jit(solution)/shard_map/all_to_all | solution.py:566
  52.6 1.1 %shard_map.91 = (f32[32,128]{1,0:T(8,128)S(1)}, f32[3,8,128]{2,1,0:T(8,128)S(1)}, f32[8,128]{1,0:T(8,128)S(1)}) custom-call(f32[32,128]{1,0:T(8,128)S(1)} %bitcast.34, f32[3,2,7,8,8,128]{5,4,3,2,1,0:T(8,128)S(1)} %get-tuple-element.44.coef_ref, f32[3,8,128]{2,1,0:T(8,128)S(1)} %get-tuple-element.45.field_ref, ...), custom_call_target="tpu_custom_call" | custom-call | flops 1000000 | bytes 1000000 | tf_op jit(solution)/shard_map/pallas_call | solution.py:554
  53.6 8.9 %all_to_all.37 = f32[32,1,128]{2,1,0:T(1,128)S(1)} all-to-all(f32[32,1,128]{2,1,0:T(1,128)S(1)} %bitcast.42), channel_id=1, replica_groups=mesh['chain'=32] {'chain'}, dimensions={0} | all-to-all | bytes 32768 | tf_op jit(solution)/shard_map/all_to_all | solution.py:566
  62.5 1.0 %shard_map.92 = (f32[32,128]{1,0:T(8,128)S(1)}, f32[8,128]{1,0:T(8,128)S(1)}, f32[8,128]{1,0:T(8,128)S(1)}, f32[8,128]{1,0:T(8,128)S(1)}) custom-call(f32[32,128]{1,0:T(8,128)S(1)} %bitcast.35, f32[200,8,128]{2,1,0:T(8,128)S(1)} %get-tuple-element.48.coef_ref, f32[8,128]{1,0:T(8,128)S(1)} %get-tuple-element.49.h_ref.rest_5_, ...), custom_call_target="tpu_custom_call" | custom-call | flops 1000000 | bytes 1000000 | tf_op jit(solution)/shard_map/pallas_call | solution.py:554
  63.5 8.9 %all_to_all.38 = f32[32,1,128]{2,1,0:T(1,128)S(1)} all-to-all(f32[32,1,128]{2,1,0:T(1,128)S(1)} %bitcast.40), channel_id=1, replica_groups=mesh['chain'=32] {'chain'}, dimensions={0} | all-to-all | bytes 32768 | tf_op jit(solution)/shard_map/all_to_all | solution.py:566
  72.4 1.1 %shard_map.93 = (f32[32,128]{1,0:T(8,128)S(1)}, f32[3,8,128]{2,1,0:T(8,128)S(1)}, f32[8,128]{1,0:T(8,128)S(1)}) custom-call(f32[32,128]{1,0:T(8,128)S(1)} %bitcast.33, f32[3,2,7,8,8,128]{5,4,3,2,1,0:T(8,128)S(1)} %get-tuple-element.44.coef_ref, f32[3,8,128]{2,1,0:T(8,128)S(1)} %get-tuple-element.45.field_ref, f32[3,8,128]{2,1,0:T(8,128)S(1)} %get-tuple-element.53.rest_0_, ...), custom_call_target="tpu_custom_call" | custom-call | flops 1000000 | bytes 1000000 | tf_op jit(solution)/shard_map/pallas_call | solution.py:554
  73.5 8.9 %all_to_all.39 = f32[32,1,128]{2,1,0:T(1,128)S(1)} all-to-all(f32[32,1,128]{2,1,0:T(1,128)S(1)} %bitcast.41), channel_id=1, replica_groups=mesh['chain'=32] {'chain'}, dimensions={0} | all-to-all | bytes 32768 | tf_op jit(solution)/shard_map/all_to_all | solution.py:566
  82.3 1.5 %shard_map.94 = (f32[32,128]{1,0:T(8,128)S(1)}, f32[8,128]{1,0:T(8,128)S(1)}) custom-call(f32[32,128]{1,0:T(8,128)S(1)} %bitcast.37, f32[200,8,128]{2,1,0:T(8,128)S(1)} %get-tuple-element.48.coef_ref, f32[8,128]{1,0:T(8,128)S(1)} %get-tuple-element.56.h_ref.rest_6_, f32[8,128]{1,0:T(8,128)S(1)} %get-tuple-element.57.w_in_ref, ...), custom_call_target="tpu_custom_call" | custom-call | flops 1000000 | bytes 1000000 | tf_op jit(solution)/shard_map/pallas_call | solution.py:554
  83.8 8.9 %all_to_all.40 = f32[32,1,128]{2,1,0:T(1,128)S(1)} all-to-all(f32[32,1,128]{2,1,0:T(1,128)S(1)} %bitcast.39), channel_id=1, replica_groups=mesh['chain'=32] {'chain'}, dimensions={0} | all-to-all | bytes 32768 | tf_op jit(solution)/shard_map/all_to_all | solution.py:566
  92.7 1.2 %shard_map.95 = (f32[4,8,128]{2,1,0:T(8,128)}, f32[4,3]{1,0:T(4,128)}) custom-call(f32[32,128]{1,0:T(8,128)S(1)} %bitcast.36, f32[3,8,128]{2,1,0:T(8,128)S(1)} %get-tuple-element.45.field_ref, f32[3,8,128]{2,1,0:T(8,128)S(1)} %get-tuple-element.53.rest_0_, f32[3,8,128]{2,1,0:T(8,128)S(1)} %get-tuple-element.60.rest_1_, ...), custom_call_target="tpu_custom_call" | custom-call | flops 1000000 | bytes 1000000 | tf_op jit(solution)/shard_map/pallas_call | solution.py:554
Async XLA Ops:
  3.0 20.6 %all-to-all-start = ((f32[32,24,128]{2,1,0:T(8,128)}), f32[32,24,128]{2,1,0:T(8,128)S(1)}, u32[]{:S(2)}, u32[]{:S(2)}) async-start(f32[32,24,128]{2,1,0:T(8,128)} %bitcast.6), calls=%async_computation | async-start | bytes 786432 | tf_op jit(solution)/shard_map/all_to_all | solution.py:566
  10.4 3.3 %collective-permute-start = (f32[776,128]{1,0:T(8,128)S(1)}, f32[776,128]{1,0:T(8,128)S(1)}, u32[]{:S(2)}, u32[]{:S(2)}) collective-permute-start(f32[776,128]{1,0:T(8,128)S(1)} %get-tuple-element.39), channel_id=1, source_target_pairs={{0,1},{1,0},{2,3},{3,2},{4,5},{5,4},{6,7},{7,6},{8,9},{9,8},{10,11... | collective-permute-start | bytes 1191944 | tf_op jit(solution)/shard_map/ppermute | solution.py:581
  10.7 3.0 %collective-permute-start.1 = (f32[776,128]{1,0:T(8,128)S(1)}, f32[776,128]{1,0:T(8,128)S(1)}, u32[]{:S(2)}, u32[]{:S(2)}) collective-permute-start(f32[776,128]{1,0:T(8,128)S(1)} %get-tuple-element.39), channel_id=1, source_target_pairs={{1,2},{2,1},{3,4},{4,3},{5,6},{6,5},{7,8},{8,7},{9,10},{10,9},{11,... | collective-permute-start | bytes 1191944 | tf_op jit(solution)/shard_map/ppermute | solution.py:580

commit v4 on v3

--- a/solution.py
+++ b/solution.py
@@ -14,7 +14,7 @@
 EPS = 1e-06
 AXIS = "chain"
 SUB = 8
-EARLY = 6
+EARLY = 5
 
 
 def padded_2(x, sides, width):
@@ -107,20 +107,17 @@
         self.far = [k for k in range(depth) if rows <= 2**k < rows * devices]
         self.sent = len(self.near) - 1
         self.count = SUB * rows * devices
-        n = len(self.far)
-        self.own_mats = 2 * n + 4
-        self.halo_mats = 2 * n + 1
+        n = len(self.far) - 1
+        self.halo_mats = 2 * n + 2
+        self.own_mats = self.halo_mats + 3
         self.own_tiles = self.own_mats * SUB
         self.halo_tiles = self.halo_mats * SUB
-        self.halo_packed = self.halo_tiles // 2
-        self.coef_tiles = self.own_tiles + self.halo_packed
+        self.coef_tiles = self.own_tiles + self.halo_tiles // 2
         self.per_group = rows // SUB
-        tiles = self.coef_tiles + 4
-        groups = -(-tiles // self.per_group)
-        step = max(1, SUB // self.piece)
-        self.groups = -(-groups // step) * step
-        self.whole_groups = self.coef_tiles // self.per_group
-        self.early = self.whole_groups * EARLY // 8 // step * step
+        self.groups = -(-self.coef_tiles // self.per_group)
+        self.early = self.groups * EARLY // 9
+        self.early_rows = self.early * self.piece
+        self.late_rows = (self.groups - self.early) * self.piece + 1
         self.width = rows // self.piece
 
 
@@ -145,24 +142,31 @@
     return jnp.sum(jnp.sum(x, axis=0, keepdims=True), axis=1, keepdims=True)
 
 
-def send(plan, tiles, z_ref, out_ref):
-    r = plan.rows
-    stacked = jnp.concatenate(tiles + [jnp.zeros((r - SUB * len(tiles), r), jnp.float32)], 0)
-    z_ref[...] = stacked.T
+def send(plan, tiles, z_ref, row=None):
+    n = plan.width - SUB * len(tiles)
+    filler = [jnp.zeros((n, plan.rows), jnp.float32)] if n else []
+    z_ref[...] = jnp.concatenate((tiles + filler) * plan.piece, 0).T
+    group = lane((plan.devices, plan.rows)) // plan.width
     out = z_ref[pl.ds(0, plan.devices, stride=plan.piece), :]
     for i in range(1, plan.piece):
         part = z_ref[pl.ds(i, plan.devices, stride=plan.piece), :]
-        out = out + pltpu.roll(part, i * plan.width, 1)
-    out_ref[...] = out
-
-
-def receive(plan, in_ref, z_ref):
-    got = in_ref[...]
+        out = jnp.where(group == i, part, out)
+    return out if row is None else out + row
+
+
+def receive(plan, got, z_ref):
     for i in range(plan.piece):
-        part = got if i == 0 else pltpu.roll(got, plan.rows - i * plan.width, 1)
-        z_ref[pl.ds(i, plan.devices, stride=plan.piece), :] = part
+        z_ref[pl.ds(i, plan.devices, stride=plan.piece), :] = got
     t = z_ref[...].T
-    return [t[SUB * k : SUB * k + SUB] for k in range(4)]
+    pos = lane() % plan.piece
+    tiles = []
+    for k in range(4):
+        at = SUB * k
+        tile = t[at : at + SUB]
+        for i in range(1, plan.piece):
+            tile = jnp.where(pos == i, t[i * plan.width + at : i * plan.width + at + SUB], tile)
+        tiles.append(tile)
+    return tiles
 
 
 def halo_of(plan, y):
@@ -210,15 +214,17 @@
 
 
 def load_kernel(plan, *refs):
-    count = (len(refs) - 2) // 2
-    ins, outs, edge_ref, sems = refs[:count], refs[count:-2], refs[-2], refs[-1]
+    count = (len(refs) - 3) // 2
+    ins, outs, edge_refs, sems = refs[:count], refs[count:-3], refs[-3:-1], refs[-1]
     rhs_ref, lo_ref, up_ref = ins[:3]
     n = 64 * plan.sent
-    pairs = [
-        (lo_ref.at[pl.ds(0, n)], edge_ref.at[pl.ds(0, n)]),
-        (up_ref.at[pl.ds(0, n)], edge_ref.at[pl.ds(n, n)]),
-        (rhs_ref, edge_ref.at[pl.ds(2 * n, SUB)]),
-    ]
+    pairs = []
+    for edge_ref in edge_refs:
+        pairs += [
+            (lo_ref.at[pl.ds(0, n)], edge_ref.at[pl.ds(0, n)]),
+            (up_ref.at[pl.ds(0, n)], edge_ref.at[pl.ds(n, n)]),
+            (rhs_ref, edge_ref.at[pl.ds(2 * n, SUB)]),
+        ]
     pairs += list(zip(ins, outs))
     copies = [pltpu.make_async_copy(x, y, sems.at[i]) for i, (x, y) in enumerate(pairs)]
     for c in copies:
@@ -227,44 +233,47 @@
         c.wait()
 
 
-def pack_tile(plan, raw, index):
-    if index < plan.own_tiles:
-        return raw(index)
-    j = 2 * (index - plan.own_tiles)
-    a, b = halo_of(plan, raw(j)), halo_of(plan, raw(j + 1))
-    pos = lane() % plan.piece
-    moved = jnp.where(pos == 1, pltpu.roll(b, 1, 1), pltpu.roll(b, plan.rows - 1, 1))
-    return jnp.where((pos == 0) | (pos == plan.piece - 1), a, moved)
-
-
-def pack_group(plan, at, rows, tiles, z_ref, slot, out_ref):
-    z_ref[slot] = jnp.concatenate(tiles, 0).T
-    for i in range(plan.piece):
-        out_ref[pl.ds(at * plan.piece + i, plan.devices, stride=rows), :] = z_ref[
-            slot, pl.ds(i, plan.devices, stride=plan.piece), :
-        ]
-
-
-def pack_kernel(plan, first, last, lo_ref, up_ref, fin_ref, dia_ref, bel_ref, abo_ref, out_ref, *rest):
-    z_ref = rest[-1]
-    mats = [(lo_ref, 64 * k) for k in plan.far] + [(up_ref, 64 * k) for k in plan.far]
+def take_kernel(in_ref, out_ref):
+    out_ref[...] = in_ref[...]
+
+
+def pack_kernel(plan, first, last, lo_ref, up_ref, fin_ref, dia_ref, bel_ref, abo_ref, out_ref, z_ref):
+    half = lax.axis_index(AXIS) >= plan.devices // 2
+    *most, top = plan.far
+    mats = [(lo_ref, 64 * k) for k in most] + [(up_ref, 64 * k) for k in most] + [None]
     mats += [(fin_ref, 0), (dia_ref, 0), (bel_ref, 0), (abo_ref, 0)]
 
     def raw(index):
-        ref, base = mats[index // SUB]
-        return ref[pl.ds(base + index % SUB, SUB, stride=SUB), :]
+        mat, b = divmod(index, SUB)
+        if mats[mat] is None:
+            low, high = (ref[pl.ds(64 * top + b, SUB, stride=SUB), :] for ref in (lo_ref, up_ref))
+            return jnp.where(half, low, high)
+        ref, base = mats[mat]
+        return ref[pl.ds(base + b, SUB, stride=SUB), :]
+
+    def tile(index):
+        if index < plan.own_tiles:
+            return raw(index)
+        if index >= plan.coef_tiles:
+            return jnp.zeros((SUB, plan.rows), jnp.float32)
+        j = 2 * (index - plan.own_tiles)
+        a, b = halo_of(plan, raw(j)), halo_of(plan, raw(j + 1))
+        pos = lane() % plan.piece
+        moved = jnp.where(pos == 1, pltpu.roll(b, 1, 1), pltpu.roll(b, plan.rows - 1, 1))
+        return jnp.where((pos == 0) | (pos == plan.piece - 1), a, moved)
 
     t = plan.per_group
     rows = out_ref.shape[0] // plan.devices
-    for g in range(first, last):
-        pack_group(plan, g - first, rows, [pack_tile(plan, raw, g * t + i) for i in range(t)], z_ref, g - first, out_ref)
-    if len(rest) > 1:
-        for i in range(last * t, plan.coef_tiles):
-            rest[0][i - last * t] = pack_tile(plan, raw, i)
+    for slot, g in enumerate(range(first, last)):
+        z_ref[slot] = jnp.concatenate([tile(g * t + i) for i in range(t)], 0).T
+        for i in range(plan.piece):
+            out_ref[pl.ds(slot * plan.piece + i, plan.devices, stride=rows), :] = z_ref[
+                slot, pl.ds(i, plan.devices, stride=plan.piece), :
+            ]
 
 
 def first_kernel(
-    plan, lo_ref, up_ref, rhs_ref, pair_ref, other_ref, rest_in_ref, chunk_ref, out_ref, coef_ref, field_ref, z_ref
+    plan, lo_ref, up_ref, rhs_ref, pair_ref, other_ref, late_ref, out_ref, coef_ref, field_ref, z_ref
 ):
     n = 64 * 2 * plan.sent
     odd = lax.rem(lax.axis_index(AXIS), 2) == 1
@@ -287,19 +296,13 @@
     for t in range(3):
         field_ref[t] = fields[t]
     y = near_levels(plan, fields, coef)
-    t = plan.per_group
-    first = plan.whole_groups * t
-    tiles = [rest_in_ref[i] for i in range(plan.coef_tiles - first)]
-    tiles += [y, halo_of(plan, y), square_tile(rhs), rhs]
-    tiles += [jnp.zeros_like(rhs)] * (plan.groups * t - first - len(tiles))
-    rows = out_ref.shape[0] // plan.devices
-    for g in range(plan.whole_groups, plan.groups):
-        at, slot = g * t - first, g - plan.whole_groups
-        pack_group(plan, g - plan.early, rows, tiles[at : at + t], z_ref, slot, out_ref)
+    out_ref[pl.ds(plan.late_rows - 1, plan.devices, stride=plan.late_rows), :] = send(
+        plan, [y, halo_of(plan, y), square_tile(rhs), rhs], z_ref
+    )
 
 
 def far_stage(plan, own, halo, coef_ref):
-    q, r, n = plan.piece, plan.rows, len(plan.far)
+    q, r, n = plan.piece, plan.rows, len(plan.far) - 1
     base = plan.own_tiles
 
     def apply(mat, x, start):
@@ -316,13 +319,14 @@
             high = apply(n + k, pltpu.roll(x, r - by, 1), start)
             fresh.append(x + low + high)
         own, halo = fresh
-    own = own + apply(2 * n, own, 0)
-    halo = wrapped(plan, halo + apply(2 * n, halo, base))
+    own, halo = (x + apply(2 * n, pltpu.roll(x, r // 2, 1), start) for x, start in ((own, 0), (halo, base)))
+    own = own + apply(2 * n + 1, own, 0)
+    halo = wrapped(plan, halo + apply(2 * n + 1, halo, base))
     pos = lane() % q
     before = jnp.where(pos == 0, halo, pltpu.roll(own, 1, 1))
     after = jnp.where(pos == q - 1, halo, pltpu.roll(own, r - 1, 1))
-    w = 2.0 * own + apply(2 * n + 1, own, 0)
-    return w + apply(2 * n + 2, before, 0) + apply(2 * n + 3, after, 0)
+    w = 2.0 * own + apply(2 * n + 2, own, 0)
+    return w + apply(2 * n + 3, before, 0) + apply(2 * n + 4, after, 0)
 
 
 def norm_of(plan, squares):
@@ -332,7 +336,7 @@
 
 
 def finish_far(plan, y, halo, s, vs, coef_ref, z_ref, out_ref):
-    w = far_stage(plan, y / s, halo / s, coef_ref)
+    w = far_stage(plan, y, halo, coef_ref) / s
     q, r = plan.piece, plan.rows
     at = lane()
     before = jnp.where(at < q, 0.0, pltpu.roll(w, q, 1))
@@ -340,7 +344,7 @@
     dots = jnp.zeros_like(w)
     for i, v in enumerate(vs):
         dots = jnp.where(sub() == i, jnp.broadcast_to(total(v * w), w.shape), dots)
-    send(plan, [before, w, after, dots], z_ref, out_ref)
+    out_ref[...] = send(plan, [before, w, after, dots], z_ref)
     return w
 
 
@@ -386,6 +390,15 @@
 def products():
     out = [(i, None) for i in range(ITERS)] + [(None, None)]
     return out + [(i, j) for i in range(ITERS) for j in range(i, ITERS)]
+
+
+def rows_sum(pair):
+    parts = [tuple(x[SUB * i : SUB * i + SUB] for x in pair) for i in range(pair[0].shape[0] // SUB)]
+    while len(parts) > 1:
+        half = len(parts) // 2
+        parts = [pair_add(a, b) for a, b in zip(parts[:half], parts[half:])]
+    one = folded(parts[0], (4, 2, 1), 0)
+    return tuple(x[0:1] for x in one)
 
 
 def last_far_kernel(plan, in_ref, coef_ref, h_ref, w_in_ref, *rest):
@@ -395,49 +408,45 @@
     y, halo, s, v = enter_far(plan, in_ref, h_ref, w_in_ref, vs, zr_ref)
     s_ref[...] = s
     vs = vs + [v]
-    w = far_stage(plan, y / s, halo / s, coef_ref)
-    sums = []
-    for a, b in products():
+    w = far_stage(plan, y, halo, coef_ref) / s
+    at = sub((2 * SUB, plan.rows))
+    packed = [jnp.zeros((2 * SUB, plan.rows), jnp.float32)] * 2
+    for i, (a, b) in enumerate(products()):
         pair = two_prod(w if a is None else vs[a], w if b is None else vs[b])
-        sums.append(folded(pair, (4, 2, 1), 0))
-    at = sub()
-    packed = []
-    for start in range(0, len(sums), SUB):
-        tile = [jnp.zeros_like(w), jnp.zeros_like(w)]
-        for i, pair in enumerate(sums[start : start + SUB]):
-            tile = [jnp.where(at == i, x, old) for x, old in zip(pair, tile)]
-        packed.append(folded(tile, [2**i for i in range(plan.rows.bit_length() - 1)], 1))
-    (hi, lo), (hi2, lo2) = packed
-    last = jnp.where(at < SUB // 2, hi2, pltpu.roll(lo2, SUB // 2, 0))
-    send(plan, [w, hi, lo, last], zs_ref, out_ref)
-
-
-def start_far_kernel(plan, early_ref, late_ref, out_ref, coef_ref, w_ref, v_ref, s_ref, z_ref, zs_ref):
+        pair = folded(pair, (4, 2, 1), 0)
+        packed = [jnp.where(at == i, jnp.concatenate([x, x], 0), old) for x, old in zip(pair, packed)]
+    filler = jnp.zeros((plan.rows - 2 * SUB, plan.rows), jnp.float32)
+    hi, lo = rows_sum(tuple(jnp.concatenate([x, filler], 0).T for x in packed))
+    hi, lo = (jnp.concatenate([x] * SUB, 0) for x in (hi, lo))
+    row = pltpu.roll(hi, SUB, 1) + pltpu.roll(lo, SUB + len(products()), 1)
+    out_ref[...] = send(plan, [w], zs_ref, row[0:1])
+
+
+def start_far_kernel(plan, early_ref, late_ref, out_ref, coef_ref, w_ref, v_ref, s_ref, z_ref, zr_ref, zs_ref):
     q, r = plan.piece, plan.rows
     at = lane()
     pos = at % q
-    n = len(plan.far)
-    g_tiles = plan.per_group
-    extra = []
+    n = len(plan.far) - 1
+
+    def limited(x, mat):
+        if mat < n:
+            return jnp.where(at < q * 2**mat, 0.0, x)
+        if mat < 2 * n:
+            return jnp.where(at >= r - q * 2 ** (mat - n), 0.0, x)
+        return x
+
     for g in range(plan.groups):
-        in_ref, at_group = (early_ref, g) if g < plan.early else (late_ref, g - plan.early)
-        rows = in_ref.shape[0] // plan.devices
+        in_ref, slot, rows = (early_ref, g, plan.early_rows)
+        if g >= plan.early:
+            in_ref, slot, rows = (late_ref, g - plan.early, plan.late_rows)
         for i in range(q):
             z_ref[g, pl.ds(i, plan.devices, stride=q), :] = in_ref[
-                pl.ds(at_group * q + i, plan.devices, stride=rows), :
+                pl.ds(slot * q + i, plan.devices, stride=rows), :
             ]
         t = z_ref[g].T
-        for j in range(g_tiles):
-            index = g * g_tiles + j
+        for j in range(plan.per_group):
+            index = g * plan.per_group + j
             tile = t[SUB * j : SUB * j + SUB]
-
-            def limited(x, mat):
-                if mat < n:
-                    return jnp.where(at < q * 2**mat, 0.0, x)
-                if mat < 2 * n:
-                    return jnp.where(at >= r - q * 2 ** (mat - n), 0.0, x)
-                return x
-
             if index < plan.own_tiles:
                 coef_ref[index] = limited(tile, index // SUB)
             elif index < plan.coef_tiles:
@@ -445,9 +454,8 @@
                 other = jnp.where(pos == 0, pltpu.roll(tile, r - 1, 1), pltpu.roll(tile, 1, 1))
                 coef_ref[plan.own_tiles + k] = limited(tile, k // SUB)
                 coef_ref[plan.own_tiles + k + 1] = limited(other, (k + 1) // SUB)
-            elif index < plan.coef_tiles + 4:
-                extra.append(tile)
-    y, halo, squares, rhs = extra
+    got = late_ref[pl.ds(plan.late_rows - 1, plan.devices, stride=plan.late_rows), :]
+    y, halo, squares, rhs = receive(plan, got, zr_ref)
     s = norm_of(plan, squares)
     v = rhs / s
     v_ref[...] = v
@@ -458,7 +466,7 @@
 def near_kernel(plan, j, in_ref, coef_ref, field_ref, *rest):
     us, ss = rest[: j - 1], rest[j - 1 : 2 * j - 1]
     out_ref, u_ref, h_ref, zr_ref, zs_ref = rest[2 * j - 1 :]
-    *w, dots = receive(plan, in_ref, zr_ref)
+    *w, dots = receive(plan, in_ref[...], zr_ref)
     pos = lane() % plan.piece
     h = jnp.sum(jnp.where(pos == 0, dots, 0.0), axis=1, keepdims=True) / plan.count
     h = jnp.broadcast_to(h, dots.shape)
@@ -472,11 +480,11 @@
         w[t] = w[t] - acc
         u_ref[t] = w[t]
     y = near_levels(plan, w, lambda t, side, k, b: coef_ref[t, side, k, b])
-    send(plan, [y, halo_of(plan, y), square_tile(w[1])], zs_ref, out_ref)
+    out_ref[...] = send(plan, [y, halo_of(plan, y), square_tile(w[1])], zs_ref)
 
 
 def enter_far(plan, in_ref, h_ref, w_in_ref, vs, z_ref):
-    y, halo, squares, _ = receive(plan, in_ref, z_ref)
+    y, halo, squares, _ = receive(plan, in_ref[...], z_ref)
     s = norm_of(plan, squares)
     h = h_ref[...]
     acc = None
@@ -500,12 +508,12 @@
     ss = [s[...] for s in rest[ITERS - 1 : 2 * ITERS - 1]]
     hs = [h[...] for h in rest[2 * ITERS - 1 : 3 * ITERS - 2]]
     basis_ref, hess_ref, z_ref = rest[3 * ITERS - 2 :]
-    w, hi, lo, last = receive(plan, in_ref, z_ref)
-    shifts = [plan.piece * 2**i for i in range(plan.devices.bit_length() - 1)]
-    one = folded((hi, lo), shifts, 1)
-    two = folded((last, pltpu.roll(last, SUB // 2, 0)), shifts, 1)
-    sums = [tuple(x[i : i + 1] for x in one) for i in range(SUB)]
-    sums += [tuple(x[i : i + 1] for x in two) for i in range(SUB // 2)]
+    raw = in_ref[...]
+    low = pltpu.roll(raw, plan.rows - len(products()), 1)
+    row = rows_sum((raw, low))
+    w = receive(plan, in_ref[...], z_ref)[0]
+    wide = lambda x: jnp.broadcast_to(x, (SUB, plan.rows))
+    sums = [tuple(wide(x[:, SUB + i : SUB + i + 1]) for x in row) for i in range(len(products()))]
     names = products()
     got = dict(zip(names, sums))
     h = [got[i, None][0] / plan.count for i in range(ITERS)]
@@ -517,20 +525,19 @@
             left = pair_add(left, pair_mul((-h[j], zero), got[min(i, j), max(i, j)]))
         squares = pair_add(squares, pair_mul((-h[i], zero), left))
     squares = jnp.maximum(squares[0], 0.0)
-    wide = lambda x: jnp.broadcast_to(x, (SUB, plan.rows))
-    ss.append(wide(jnp.sqrt(squares / plan.count + EPS)))
+    ss.append(jnp.sqrt(squares / plan.count + EPS))
     fields = [field_ref[1]] + [u[1] for u in us]
     vs = [f / s for f, s in zip(fields, ss)]
     acc = None
     for i in range(ITERS):
-        term = wide(h[i]) * vs[i]
+        term = h[i] * vs[i]
         acc = term if acc is None else acc + term
     vs.append((w - acc) / ss[-1])
     for j in range(ITERS + 1):
         basis_ref[j] = vs[j]
     top = jnp.zeros_like(w)
     for i in range(ITERS):
-        top = jnp.where(sub() == i, wide(h[i]), top)
+        top = jnp.where(sub() == i, h[i], top)
     hs.append(top)
     hess = jnp.zeros_like(w)
     for j in range(ITERS):
@@ -563,53 +570,53 @@
         )(*args)
 
     def exchange(x):
-        y = lax.all_to_all(x.reshape(d, -1, r), AXIS, 0, 0)
+        y = lax.all_to_all(x.reshape(-1, 1, r), AXIS, 0, 0, tiled=True)
         return y.reshape(-1, r)
 
     part = functools.partial
     raw = tuple(pltpu.with_memory_space_constraint(x, pltpu.HBM) for x in (right_side, lo, up, fin, dia, bel, abo))
-    *loaded, edge = call(
+    edge = shape(64 * 2 * plan.sent + SUB, r)
+    *loaded, edge_across, edge_pair = call(
         part(load_kernel, plan),
-        (*(shape(*x.shape) for x in raw), shape(64 * 2 * plan.sent + SUB, r)),
-        [pltpu.SemaphoreType.DMA((len(raw) + 3,))],
+        (*(shape(*x.shape) for x in raw), edge, edge),
+        [pltpu.SemaphoreType.DMA((len(raw) + 6,))],
         *raw,
         space=pltpu.HBM,
     )
     rhs, lo, up = loaded[:3]
     mats = loaded[1:]
-    other = lax.ppermute(edge, AXIS, [(i, i + 1 if i % 2 else i - 1) for i in range(1, d - 1)])
-    pair = lax.ppermute(edge, AXIS, [(i, i ^ 1) for i in range(d)])
-    rows_of = lambda groups: d * groups * plan.piece
+    other = lax.ppermute(edge_across, AXIS, [(i, i + 1 if i % 2 else i - 1) for i in range(1, d - 1)])
+    pair = lax.ppermute(edge_pair, AXIS, [(i, i ^ 1) for i in range(d)])
+    pair = call(take_kernel, edge, [], pair)
     early = call(
         part(pack_kernel, plan, 0, plan.early),
-        shape(rows_of(plan.early), r),
+        shape(d * plan.early_rows, r),
         [scratch(plan.early, r, r)],
         *mats,
         flops=10_000_000,
     )
     early = exchange(early)
-    left = plan.coef_tiles - plan.whole_groups * plan.per_group
-    late_shape = shape(rows_of(plan.groups - plan.early), r)
-    late, rest = call(
-        part(pack_kernel, plan, plan.early, plan.whole_groups),
-        (late_shape, shape(max(left, 1), SUB, r)),
-        [scratch(plan.whole_groups - plan.early, r, r)],
+    late_shape = shape(d * plan.late_rows, r)
+    late = call(
+        part(pack_kernel, plan, plan.early, plan.groups),
+        late_shape,
+        [scratch(plan.groups - plan.early, r, r)],
         *mats,
         flops=10_000_000,
     )
     late, near, fields = call(
         part(first_kernel, plan),
         (late_shape, shape(3, 2, len(plan.near), SUB, SUB, r), shape(3, SUB, r)),
-        [scratch(plan.groups - plan.whole_groups, r, r)],
-        lo, up, rhs, pair, other, rest, late,
-        input_output_aliases={6: 0},
+        [scratch(r, r)],
+        lo, up, rhs, pair, other, late,
+        input_output_aliases={5: 0},
     )
     small = shape(d, r)
     two = [scratch(r, r), scratch(r, r)]
     out, coef, w, v, s = call(
         part(start_far_kernel, plan),
         (small, shape(plan.own_tiles + plan.halo_tiles, SUB, r), tile, tile, tile),
-        [scratch(plan.groups, r, r), scratch(r, r)],
+        [scratch(plan.groups, r, r), *two],
         early, exchange(late),
     )
     us, ss, vs, hs = [], [s], [v], []

time: 94.2 us -> 92.8 us (0.985)
  Pallas kernels: 12.4 us -> 10.6 us
  blocking collectives: 63.3 us -> 64.4 us
    pallas_call x10 -> x11, Pallas kernels: 12.4 us -> 10.6 us  [call(): pl.pallas_call(kernel, out_shape=outs, in_specs=[pl.BlockSpec(memory_spac...]
    all_to_all x6, blocking collectives: 63.3 us -> 64.4 us  [exchange(): y = lax.all_to_all(x.reshape(-1, 1, r), AXIS, 0, 0, tiled=True)]
where the time goes in v4:
time: 92.8 us; the launch traced here: 92.5 us
  blocking collectives  64.4 us (69%)
  Pallas kernels  10.6 us (11%)
  waiting for transfers between devices  8.44 us (9%)
  starting transfers between devices  8.32 us (9%)
    all_to_all x6, blocking collectives, exchange(): y = lax.all_to_all(x.reshape(-1, 1, r), AXIS, 0, 0, tiled=True)  64.4 us
    pallas_call x11, Pallas kernels, call(): pl.pallas_call(kernel, out_shape=outs, in_specs=[pl.BlockSpec(memory_spac...  10.6 us
    all_to_all x1, waiting for transfers between devices, exchange(): y = lax.all_to_all(x.reshape(-1, 1, r), AXIS, 0, 0, tiled=True)  8.43 us
    all_to_all x1, starting transfers between devices, exchange(): y = lax.all_to_all(x.reshape(-1, 1, r), AXIS, 0, 0, tiled=True)  7.33 us
  transfers between devices with their start and end apart: 3, of which 1 were waited for; matrix products, arithmetic and copies ran while one was open for 0% of the time, Pallas kernels for 3%

profile of v4, /device:TPU:0, one launch (start us, length us, event | category | flops | bytes accessed | tf_op | source)
XLA Modules:
  0.0 92.5 jit_solution(14209977738515538986)
XLA Ops:
  0.6 1.7 %shard_map.86 = (f32[8,128]{1,0:T(8,128)S(1)}, f32[768,128]{1,0:T(8,128)S(1)}, f32[768,128]{1,0:T(8,128)S(1)}, f32[64,128]{1,0:T(8,128)S(1)}, f32[64,128]{1,0:T(...) custom-call(f32[8,128]{1,0:T(8,128)} %refs_0_.1, ...), custom_call_target="tpu_custom_call" | custom-call | flops 1000000 | bytes 1000000 | tf_op jit(solution)/shard_map/pallas_call | solution.py:561
  2.3 0.9 shard_map.87
  3.2 7.3 %all-to-all-start = ((f32[640,1,128]{2,1,0:T(1,128)}), f32[640,1,128]{2,1,0:T(1,128)S(1)}, u32[]{:S(2)}, u32[]{:S(2)}) async-start(f32[640,1,128]{2,1,0:T(1,128)} %bitcast.7), calls=%async_computation | async-start | bytes 655360 | tf_op jit(solution)/shard_map/all_to_all | solution.py:573
  10.6 0.3 collective-permute-start
  10.9 0.7 collective-permute-start.1
  11.6 1.8 %shard_map.89.late_ref = f32[544,128]{1,0:T(8,128)S(1)} custom-call(f32[768,128]{1,0:T(8,128)S(1)} %get-tuple-element.31.lo_ref, f32[768,128]{1,0:T(8,128)S(1)} %get-tuple-element.32.up_ref, f32[64,128]{1,0:T(8,128)S(1)} %get-tuple-element.33.fin_ref, f32[64,128]{1,0:T(8,128)S(1)} %get-tuple-element.34.dia_ref, f32[64,128]{1,0:T(8,128)S(1)} %get-tuple-element.35.bel_ref, ...), custom_call_target="tpu_custom_call" | custom-call | flops 10000000 | bytes 1000000 | tf_op jit(solution)/shard_map/pallas_call | solution.py:561
  13.3 0.0 collective-permute-done.in_ref
  13.4 0.0 collective-permute-done.1.other_ref
  13.4 0.8 shard_map.90
  14.2 8.4 %all-to-all-done = f32[640,1,128]{2,1,0:T(1,128)S(1)} async-done(((f32[640,1,128]{2,1,0:T(1,128)}), f32[640,1,128]{2,1,0:T(1,128)S(1)}, u32[]{:S(2)}, u32[]{:S(2)}) %all-to-all-start) | async-done | bytes 327712 | tf_op jit(solution)/shard_map/all_to_all | solution.py:573
  22.6 19.7 %all_to_all.35 = f32[544,1,128]{2,1,0:T(1,128)S(1)} all-to-all(f32[544,1,128]{2,1,0:T(1,128)S(1)} %bitcast.34), channel_id=1, replica_groups=mesh['chain'=32] {'chain'}, dimensions={0} | all-to-all | bytes 557056 | tf_op jit(solution)/shard_map/all_to_all | solution.py:573
  42.3 1.0 %shard_map.91 = (f32[32,128]{1,0:T(8,128)S(1)}, f32[184,8,128]{2,1,0:T(8,128)S(1)}, f32[8,128]{1,0:T(8,128)S(1)}, f32[8,128]{1,0:T(8,128)S(1)}, f32[8,128]{1,0:T(8,128)S(1)}) custom-call(f32[640,128]{1,0:T(8,128)S(1)} %bitcast.35, f32[544,128]{1,0:T(8,128)S(1)} %bitcast.36), custom_call_target="tpu_custom_call" | custom-call | flops 1000000 | bytes 1000000 | tf_op jit(solution)/shard_map/pallas_call | solution.py:561
  43.3 9.2 %all_to_all.36 = f32[32,1,128]{2,1,0:T(1,128)S(1)} all-to-all(f32[32,1,128]{2,1,0:T(1,128)S(1)} %bitcast.42), channel_id=1, replica_groups=mesh['chain'=32] {'chain'}, dimensions={0} | all-to-all | bytes 32768 | tf_op jit(solution)/shard_map/all_to_all | solution.py:573
  52.5 1.0 %shard_map.92 = (f32[32,128]{1,0:T(8,128)S(1)}, f32[3,8,128]{2,1,0:T(8,128)S(1)}, f32[8,128]{1,0:T(8,128)S(1)}) custom-call(f32[32,128]{1,0:T(8,128)S(1)} %bitcast.38, f32[3,2,7,8,8,128]{5,4,3,2,1,0:T(8,128)S(1)} %get-tuple-element.42.coef_ref, f32[3,8,128]{2,1,0:T(8,128)S(1)} %get-tuple-element.43.field_ref, ...), custom_call_target="tpu_custom_call" | custom-call | flops 1000000 | bytes 1000000 | tf_op jit(solution)/shard_map/pallas_call | solution.py:561
  53.5 8.9 %all_to_all.37 = f32[32,1,128]{2,1,0:T(1,128)S(1)} all-to-all(f32[32,1,128]{2,1,0:T(1,128)S(1)} %bitcast.46), channel_id=1, replica_groups=mesh['chain'=32] {'chain'}, dimensions={0} | all-to-all | bytes 32768 | tf_op jit(solution)/shard_map/all_to_all | solution.py:573
  62.3 0.8 shard_map.93
  63.1 8.9 %all_to_all.38 = f32[32,1,128]{2,1,0:T(1,128)S(1)} all-to-all(f32[32,1,128]{2,1,0:T(1,128)S(1)} %bitcast.44), channel_id=1, replica_groups=mesh['chain'=32] {'chain'}, dimensions={0} | all-to-all | bytes 32768 | tf_op jit(solution)/shard_map/all_to_all | solution.py:573
  72.0 1.0 %shard_map.94 = (f32[32,128]{1,0:T(8,128)S(1)}, f32[3,8,128]{2,1,0:T(8,128)S(1)}, f32[8,128]{1,0:T(8,128)S(1)}) custom-call(f32[32,128]{1,0:T(8,128)S(1)} %bitcast.37, f32[3,2,7,8,8,128]{5,4,3,2,1,0:T(8,128)S(1)} %get-tuple-element.42.coef_ref, f32[3,8,128]{2,1,0:T(8,128)S(1)} %get-tuple-element.43.field_ref, f32[3,8,128]{2,1,0:T(8,128)S(1)} %get-tuple-element.51.rest_0_, ...), custom_call_target="tpu_custom_call" | custom-call | flops 1000000 | bytes 1000000 | tf_op jit(solution)/shard_map/pallas_call | solution.py:561
  73.0 8.9 %all_to_all.39 = f32[32,1,128]{2,1,0:T(1,128)S(1)} all-to-all(f32[32,1,128]{2,1,0:T(1,128)S(1)} %bitcast.45), channel_id=1, replica_groups=mesh['chain'=32] {'chain'}, dimensions={0} | all-to-all | bytes 32768 | tf_op jit(solution)/shard_map/all_to_all | solution.py:573
  81.8 0.9 shard_map.95
  82.7 8.9 %all_to_all.40 = f32[32,1,128]{2,1,0:T(1,128)S(1)} all-to-all(f32[32,1,128]{2,1,0:T(1,128)S(1)} %bitcast.43), channel_id=1, replica_groups=mesh['chain'=32] {'chain'}, dimensions={0} | all-to-all | bytes 32768 | tf_op jit(solution)/shard_map/all_to_all | solution.py:573
  91.6 0.9 shard_map.96
  (1 shorter events, 0.0 us)
Async XLA Ops:
  3.2 19.4 %all-to-all-start = ((f32[640,1,128]{2,1,0:T(1,128)}), f32[640,1,128]{2,1,0:T(1,128)S(1)}, u32[]{:S(2)}, u32[]{:S(2)}) async-start(f32[640,1,128]{2,1,0:T(1,128)} %bitcast.7), calls=%async_computation | async-start | bytes 655360 | tf_op jit(solution)/shard_map/all_to_all | solution.py:573
  10.6 2.8 %collective-permute-start = (f32[776,128]{1,0:T(8,128)S(1)}, f32[776,128]{1,0:T(8,128)S(1)}, u32[]{:S(2)}, u32[]{:S(2)}) collective-permute-start(f32[776,128]{1,0:T(8,128)S(1)} %get-tuple-element.38), channel_id=1, source_target_pairs={{0,1},{1,0},{2,3},{3,2},{4,5},{5,4},{6,7},{7,6},{8,9},{9,8},{10,11... | collective-permute-start | bytes 1191944 | tf_op jit(solution)/shard_map/ppermute | solution.py:589
  10.9 2.5 %collective-permute-start.1 = (f32[776,128]{1,0:T(8,128)S(1)}, f32[776,128]{1,0:T(8,128)S(1)}, u32[]{:S(2)}, u32[]{:S(2)}) collective-permute-start(f32[776,128]{1,0:T(8,128)S(1)} %get-tuple-element.39), channel_id=1, source_target_pairs={{1,2},{2,1},{3,4},{4,3},{5,6},{6,5},{7,8},{8,7},{9,10},{10,9},{11,... | collective-permute-start | bytes 1191944 | tf_op jit(solution)/shard_map/ppermute | solution.py:588

commit v5 on v4

--- a/solution.py
+++ b/solution.py
@@ -142,16 +142,37 @@
     return jnp.sum(jnp.sum(x, axis=0, keepdims=True), axis=1, keepdims=True)
 
 
-def send(plan, tiles, z_ref, row=None):
+def send(plan, tiles, z_ref, wrap=False, row=None, sums=None):
+    q, r = plan.piece, plan.rows
     n = plan.width - SUB * len(tiles)
-    filler = [jnp.zeros((n, plan.rows), jnp.float32)] if n else []
-    z_ref[...] = jnp.concatenate((tiles + filler) * plan.piece, 0).T
-    group = lane((plan.devices, plan.rows)) // plan.width
-    out = z_ref[pl.ds(0, plan.devices, stride=plan.piece), :]
-    for i in range(1, plan.piece):
-        part = z_ref[pl.ds(i, plan.devices, stride=plan.piece), :]
-        out = jnp.where(group == i, part, out)
+    filler = [jnp.zeros((n, r), jnp.float32)] if n else []
+    z = jnp.concatenate(([t for t, _ in tiles] + filler) * q, 0).T
+    pad = jnp.zeros((SUB, r), jnp.float32)
+    z_ref[pl.ds(0, SUB), :] = z[r - SUB :] if wrap else pad
+    z_ref[pl.ds(SUB, r), :] = z
+    z_ref[pl.ds(SUB + r, SUB), :] = z[:SUB] if wrap else pad
+    place = lane((plan.devices, r)) // SUB
+    out = jnp.zeros((plan.devices, r), jnp.float32)
+    for i in range(q):
+        loads = {}
+        for k, (_, offsets) in enumerate(tiles):
+            if offsets is None or offsets[i] is None:
+                continue
+            if offsets[i] not in loads:
+                loads[offsets[i]] = z_ref[pl.ds(SUB + i + offsets[i], plan.devices, stride=q), :]
+            out = jnp.where(place == i * (plan.width // SUB) + k, loads[offsets[i]], out)
+    if sums is not None:
+        parts = [z[SUB * i : SUB * i + SUB] for i in range(r // SUB)]
+        while len(parts) > 1:
+            parts = [x + y for x, y in zip(parts[::2], parts[1::2])]
+        whole = jnp.broadcast_to(jnp.sum(parts[0], axis=0, keepdims=True), out.shape)
+        out = jnp.where(place == sums, whole, out)
     return out if row is None else out + row
+
+
+def sent_field(plan, y):
+    q = plan.piece
+    return [(y, (0,) * q), (y, (-1,) + (None,) * (q - 2) + (1,))]
 
 
 def receive(plan, got, z_ref):
@@ -216,21 +237,25 @@
 def load_kernel(plan, *refs):
     count = (len(refs) - 3) // 2
     ins, outs, edge_refs, sems = refs[:count], refs[count:-3], refs[-3:-1], refs[-1]
-    rhs_ref, lo_ref, up_ref = ins[:3]
-    n = 64 * plan.sent
-    pairs = []
-    for edge_ref in edge_refs:
-        pairs += [
-            (lo_ref.at[pl.ds(0, n)], edge_ref.at[pl.ds(0, n)]),
-            (up_ref.at[pl.ds(0, n)], edge_ref.at[pl.ds(n, n)]),
-            (rhs_ref, edge_ref.at[pl.ds(2 * n, SUB)]),
-        ]
-    pairs += list(zip(ins, outs))
-    copies = [pltpu.make_async_copy(x, y, sems.at[i]) for i, (x, y) in enumerate(pairs)]
+    copies = [pltpu.make_async_copy(x, y, sems.at[i]) for i, (x, y) in enumerate(zip(ins, outs))]
     for c in copies:
         c.start()
     for c in copies:
         c.wait()
+    rhs_ref, lo_ref, up_ref = outs[:3]
+    n = 64 * (plan.sent - 1)
+    odd = lax.rem(lax.axis_index(AXIS), 2) == 1
+    first = lane((64, plan.rows)) < plan.rows // 2
+    low = lo_ref[pl.ds(n, 64), :]
+    high = pltpu.roll(up_ref[pl.ds(n, 64), :], plan.rows // 2, 1)
+    as_prev, as_next = jnp.where(first, high, low), jnp.where(first, low, high)
+    across_ref, pair_ref = edge_refs
+    across_ref[pl.ds(2 * n, 64), :] = jnp.where(odd, as_prev, as_next)
+    pair_ref[pl.ds(2 * n, 64), :] = jnp.where(odd, as_next, as_prev)
+    for ref in edge_refs:
+        ref[pl.ds(0, n), :] = lo_ref[pl.ds(0, n), :]
+        ref[pl.ds(n, n), :] = up_ref[pl.ds(0, n), :]
+        ref[pl.ds(2 * n + 64, SUB), :] = rhs_ref[...]
 
 
 def take_kernel(in_ref, out_ref):
@@ -275,7 +300,8 @@
 def first_kernel(
     plan, lo_ref, up_ref, rhs_ref, pair_ref, other_ref, late_ref, out_ref, coef_ref, field_ref, z_ref
 ):
-    n = 64 * 2 * plan.sent
+    last = plan.sent - 1
+    n = 64 * (2 * last + 1)
     odd = lax.rem(lax.axis_index(AXIS), 2) == 1
     rhs = rhs_ref[...]
 
@@ -287,8 +313,11 @@
         if t == 1:
             ref = up_ref if side else lo_ref
             x = ref[pl.ds(64 * k + b, SUB, stride=SUB), :]
+        elif k < last:
+            x = halo(t, 64 * (last * side + k) + b, SUB)
         else:
-            x = halo(t, 64 * (plan.sent * side + k) + b, SUB)
+            x = halo(t, 64 * 2 * last + b, SUB)
+            x = pltpu.roll(x, plan.rows // 2, 1) if side else x
         coef_ref[t, side, k, b] = x
         return x
 
@@ -296,8 +325,9 @@
     for t in range(3):
         field_ref[t] = fields[t]
     y = near_levels(plan, fields, coef)
+    plain = (0,) * plan.piece
     out_ref[pl.ds(plan.late_rows - 1, plan.devices, stride=plan.late_rows), :] = send(
-        plan, [y, halo_of(plan, y), square_tile(rhs), rhs], z_ref
+        plan, [*sent_field(plan, y), (square_tile(rhs), plain), (rhs, plain)], z_ref, wrap=True
     )
 
 
@@ -337,14 +367,12 @@
 
 def finish_far(plan, y, halo, s, vs, coef_ref, z_ref, out_ref):
     w = far_stage(plan, y, halo, coef_ref) / s
-    q, r = plan.piece, plan.rows
-    at = lane()
-    before = jnp.where(at < q, 0.0, pltpu.roll(w, q, 1))
-    after = jnp.where(at >= r - q, 0.0, pltpu.roll(w, r - q, 1))
+    q = plan.piece
     dots = jnp.zeros_like(w)
     for i, v in enumerate(vs):
-        dots = jnp.where(sub() == i, jnp.broadcast_to(total(v * w), w.shape), dots)
-    out_ref[...] = send(plan, [before, w, after, dots], z_ref)
+        dots = jnp.where(sub() == i, jnp.sum(v * w, axis=0, keepdims=True), dots)
+    tiles = [(w, (by,) * q) for by in (-q, 0, q)] + [(dots, None)]
+    out_ref[...] = send(plan, tiles, z_ref, sums=3)
     return w
 
 
@@ -419,7 +447,7 @@
     hi, lo = rows_sum(tuple(jnp.concatenate([x, filler], 0).T for x in packed))
     hi, lo = (jnp.concatenate([x] * SUB, 0) for x in (hi, lo))
     row = pltpu.roll(hi, SUB, 1) + pltpu.roll(lo, SUB + len(products()), 1)
-    out_ref[...] = send(plan, [w], zs_ref, row[0:1])
+    out_ref[...] = send(plan, [(w, (0,) * plan.piece)], zs_ref, row=row[0:1])
 
 
 def start_far_kernel(plan, early_ref, late_ref, out_ref, coef_ref, w_ref, v_ref, s_ref, z_ref, zr_ref, zs_ref):
@@ -466,21 +494,24 @@
 def near_kernel(plan, j, in_ref, coef_ref, field_ref, *rest):
     us, ss = rest[: j - 1], rest[j - 1 : 2 * j - 1]
     out_ref, u_ref, h_ref, zr_ref, zs_ref = rest[2 * j - 1 :]
-    *w, dots = receive(plan, in_ref[...], zr_ref)
-    pos = lane() % plan.piece
-    h = jnp.sum(jnp.where(pos == 0, dots, 0.0), axis=1, keepdims=True) / plan.count
-    h = jnp.broadcast_to(h, dots.shape)
-    h_ref[...] = h
+    got = in_ref[...]
+    dots = jnp.sum(got, axis=0, keepdims=True) / plan.count
+    h = [jnp.broadcast_to(dots[:, 3 * SUB + i : 3 * SUB + i + 1], (SUB, plan.rows)) for i in range(j)]
+    w = receive(plan, got, zr_ref)[:3]
+    tall = jnp.zeros_like(h[0])
+    for i in range(j):
+        tall = jnp.where(sub() == i, h[i], tall)
+    h_ref[...] = tall
     fields = [field_ref, *us]
     for t in range(3):
         acc = None
         for i in range(j):
-            term = spread(h, i) * (fields[i][t] / ss[i][...])
+            term = h[i] * (fields[i][t] / ss[i][...])
             acc = term if acc is None else acc + term
         w[t] = w[t] - acc
         u_ref[t] = w[t]
     y = near_levels(plan, w, lambda t, side, k, b: coef_ref[t, side, k, b])
-    out_ref[...] = send(plan, [y, halo_of(plan, y), square_tile(w[1])], zs_ref)
+    out_ref[...] = send(plan, [*sent_field(plan, y), (square_tile(w[1]), (0,) * plan.piece)], zs_ref, wrap=True)
 
 
 def enter_far(plan, in_ref, h_ref, w_in_ref, vs, z_ref):
@@ -575,11 +606,11 @@
 
     part = functools.partial
     raw = tuple(pltpu.with_memory_space_constraint(x, pltpu.HBM) for x in (right_side, lo, up, fin, dia, bel, abo))
-    edge = shape(64 * 2 * plan.sent + SUB, r)
+    edge = shape(64 * (2 * plan.sent - 1) + SUB, r)
     *loaded, edge_across, edge_pair = call(
         part(load_kernel, plan),
         (*(shape(*x.shape) for x in raw), edge, edge),
-        [pltpu.SemaphoreType.DMA((len(raw) + 6,))],
+        [pltpu.SemaphoreType.DMA((len(raw),))],
         *raw,
         space=pltpu.HBM,
     )
@@ -607,12 +638,13 @@
     late, near, fields = call(
         part(first_kernel, plan),
         (late_shape, shape(3, 2, len(plan.near), SUB, SUB, r), shape(3, SUB, r)),
-        [scratch(r, r)],
+        [scratch(r + 2 * SUB, r)],
         lo, up, rhs, pair, other, late,
         input_output_aliases={5: 0},
     )
     small = shape(d, r)
-    two = [scratch(r, r), scratch(r, r)]
+    padded = scratch(r + 2 * SUB, r)
+    two = [scratch(r, r), padded]
     out, coef, w, v, s = call(
         part(start_far_kernel, plan),
         (small, shape(plan.own_tiles + plan.halo_tiles, SUB, r), tile, tile, tile),

time: 92.8 us -> 91.4 us (0.985)
  no operation moved by 1% of the time
where the time goes in v5:
time: 91.4 us; the launch traced here: 91 us
  blocking collectives  63.6 us (70%)
  Pallas kernels  9.81 us (11%)
  waiting for transfers between devices  8.49 us (9%)
  starting transfers between devices  8.31 us (9%)
    all_to_all x6, blocking collectives, exchange(): y = lax.all_to_all(x.reshape(-1, 1, r), AXIS, 0, 0, tiled=True)  63.6 us
    pallas_call x11, Pallas kernels, call(): pl.pallas_call(kernel, out_shape=outs, in_specs=[pl.BlockSpec(memory_spac...  9.81 us
    all_to_all x1, waiting for transfers between devices, exchange(): y = lax.all_to_all(x.reshape(-1, 1, r), AXIS, 0, 0, tiled=True)  8.48 us
    all_to_all x1, starting transfers between devices, exchange(): y = lax.all_to_all(x.reshape(-1, 1, r), AXIS, 0, 0, tiled=True)  7.33 us
  transfers between devices with their start and end apart: 3, of which 1 were waited for; matrix products, arithmetic and copies ran while one was open for 0% of the time, Pallas kernels for 3%

profile of v5, /device:TPU:0, one launch (start us, length us, event | category | flops | bytes accessed | tf_op | source)
XLA Modules:
  0.0 91.0 jit_solution(16482817640407359723)
XLA Ops:
  0.6 1.3 %shard_map.86 = (f32[8,128]{1,0:T(8,128)S(1)}, f32[768,128]{1,0:T(8,128)S(1)}, f32[768,128]{1,0:T(8,128)S(1)}, f32[64,128]{1,0:T(8,128)S(1)}, f32[64,128]{1,0:T(...) custom-call(f32[8,128]{1,0:T(8,128)} %refs_0_.1, ...), custom_call_target="tpu_custom_call" | custom-call | flops 1000000 | bytes 1000000 | tf_op jit(solution)/shard_map/pallas_call | solution.py:592
  1.9 0.9 %shard_map.87 = f32[640,128]{1,0:T(8,128)} custom-call(f32[768,128]{1,0:T(8,128)S(1)} %get-tuple-element.31.lo_ref, f32[768,128]{1,0:T(8,128)S(1)} %get-tuple-element.32.up_ref, f32[64,128]{1,0:T(8,128)S(1)} %get-tuple-element.33.fin_ref, f32[64,128]{1,0:T(8,128)S(1)} %get-tuple-element.34.dia_ref, f32[64,128]{1,0:T(8,128)S(1)} %get-tuple-element.35.bel_ref, ...), custom_call_target="tpu_custom_call" | custom-call | flops 10000000 | bytes 1000000 | tf_op jit(solution)/shard_map/pallas_call | solution.py:592
  2.9 7.3 %all-to-all-start = ((f32[640,1,128]{2,1,0:T(1,128)}), f32[640,1,128]{2,1,0:T(1,128)S(1)}, u32[]{:S(2)}, u32[]{:S(2)}) async-start(f32[640,1,128]{2,1,0:T(1,128)} %bitcast.7), calls=%async_computation | async-start | bytes 655360 | tf_op jit(solution)/shard_map/all_to_all | solution.py:604
  10.2 0.3 collective-permute-start
  10.5 0.7 collective-permute-start.1
  11.2 1.8 %shard_map.89.late_ref = f32[544,128]{1,0:T(8,128)S(1)} custom-call(f32[768,128]{1,0:T(8,128)S(1)} %get-tuple-element.31.lo_ref, f32[768,128]{1,0:T(8,128)S(1)} %get-tuple-element.32.up_ref, f32[64,128]{1,0:T(8,128)S(1)} %get-tuple-element.33.fin_ref, f32[64,128]{1,0:T(8,128)S(1)} %get-tuple-element.34.dia_ref, f32[64,128]{1,0:T(8,128)S(1)} %get-tuple-element.35.bel_ref, ...), custom_call_target="tpu_custom_call" | custom-call | flops 10000000 | bytes 1000000 | tf_op jit(solution)/shard_map/pallas_call | solution.py:592
  13.0 0.0 collective-permute-done.in_ref
  13.0 0.0 collective-permute-done.1.other_ref
  13.0 0.7 shard_map.90
  13.8 8.5 %all-to-all-done = f32[640,1,128]{2,1,0:T(1,128)S(1)} async-done(((f32[640,1,128]{2,1,0:T(1,128)}), f32[640,1,128]{2,1,0:T(1,128)S(1)}, u32[]{:S(2)}, u32[]{:S(2)}) %all-to-all-start) | async-done | bytes 327712 | tf_op jit(solution)/shard_map/all_to_all | solution.py:604
  22.2 18.9 %all_to_all.35 = f32[544,1,128]{2,1,0:T(1,128)S(1)} all-to-all(f32[544,1,128]{2,1,0:T(1,128)S(1)} %bitcast.34), channel_id=1, replica_groups=mesh['chain'=32] {'chain'}, dimensions={0} | all-to-all | bytes 557056 | tf_op jit(solution)/shard_map/all_to_all | solution.py:604
  41.1 0.9 shard_map.91
  42.1 9.2 %all_to_all.36 = f32[32,1,128]{2,1,0:T(1,128)S(1)} all-to-all(f32[32,1,128]{2,1,0:T(1,128)S(1)} %bitcast.42), channel_id=1, replica_groups=mesh['chain'=32] {'chain'}, dimensions={0} | all-to-all | bytes 32768 | tf_op jit(solution)/shard_map/all_to_all | solution.py:604
  51.3 0.8 shard_map.92
  52.1 8.9 %all_to_all.37 = f32[32,1,128]{2,1,0:T(1,128)S(1)} all-to-all(f32[32,1,128]{2,1,0:T(1,128)S(1)} %bitcast.46), channel_id=1, replica_groups=mesh['chain'=32] {'chain'}, dimensions={0} | all-to-all | bytes 32768 | tf_op jit(solution)/shard_map/all_to_all | solution.py:604
  61.0 0.7 shard_map.93
  61.7 8.9 %all_to_all.38 = f32[32,1,128]{2,1,0:T(1,128)S(1)} all-to-all(f32[32,1,128]{2,1,0:T(1,128)S(1)} %bitcast.44), channel_id=1, replica_groups=mesh['chain'=32] {'chain'}, dimensions={0} | all-to-all | bytes 32768 | tf_op jit(solution)/shard_map/all_to_all | solution.py:604
  70.6 0.8 shard_map.94
  71.4 8.9 %all_to_all.39 = f32[32,1,128]{2,1,0:T(1,128)S(1)} all-to-all(f32[32,1,128]{2,1,0:T(1,128)S(1)} %bitcast.45), channel_id=1, replica_groups=mesh['chain'=32] {'chain'}, dimensions={0} | all-to-all | bytes 32768 | tf_op jit(solution)/shard_map/all_to_all | solution.py:604
  80.3 0.9 shard_map.95
  81.2 8.9 %all_to_all.40 = f32[32,1,128]{2,1,0:T(1,128)S(1)} all-to-all(f32[32,1,128]{2,1,0:T(1,128)S(1)} %bitcast.43), channel_id=1, replica_groups=mesh['chain'=32] {'chain'}, dimensions={0} | all-to-all | bytes 32768 | tf_op jit(solution)/shard_map/all_to_all | solution.py:604
  90.1 0.9 shard_map.96
  (1 shorter events, 0.0 us)
Async XLA Ops:
  2.9 19.4 %all-to-all-start = ((f32[640,1,128]{2,1,0:T(1,128)}), f32[640,1,128]{2,1,0:T(1,128)S(1)}, u32[]{:S(2)}, u32[]{:S(2)}) async-start(f32[640,1,128]{2,1,0:T(1,128)} %bitcast.7), calls=%async_computation | async-start | bytes 655360 | tf_op jit(solution)/shard_map/all_to_all | solution.py:604
  10.2 2.8 %collective-permute-start = (f32[712,128]{1,0:T(8,128)S(1)}, f32[712,128]{1,0:T(8,128)S(1)}, u32[]{:S(2)}, u32[]{:S(2)}) collective-permute-start(f32[712,128]{1,0:T(8,128)S(1)} %get-tuple-element.38), channel_id=1, source_target_pairs={{0,1},{1,0},{2,3},{3,2},{4,5},{5,4},{6,7},{7,6},{8,9},{9,8},{10,11... | collective-permute-start | bytes 1093640 | tf_op jit(solution)/shard_map/ppermute | solution.py:620
  10.5 2.5 %collective-permute-start.1 = (f32[712,128]{1,0:T(8,128)S(1)}, f32[712,128]{1,0:T(8,128)S(1)}, u32[]{:S(2)}, u32[]{:S(2)}) collective-permute-start(f32[712,128]{1,0:T(8,128)S(1)} %get-tuple-element.39), channel_id=1, source_target_pairs={{1,2},{2,1},{3,4},{4,3},{5,6},{6,5},{7,8},{8,7},{9,10},{10,9},{11,... | collective-permute-start | bytes 1093640 | tf_op jit(solution)/shard_map/ppermute | solution.py:619
